TPU v7x, 8 devices: a whole 2x2x1 slice. The times are simulated.
8 devices in a mesh: dp: 2 (over z, y), cp: 4 (over x, core).
Axes of the slice: x: 2, y: 2, z: 1, core: 2. Of those that a mesh axis runs over, the one named last changes fastest.
Arguments:
- queries: bfloat16 [128, 128, 128], P(('dp', 'cp')), parts along dimension 0
- key_new: bfloat16 [128, 8, 128], P(('dp', 'cp')), parts along dimension 0
- value_new: bfloat16 [128, 8, 128], P(('dp', 'cp')), parts along dimension 0
- key_cache: bfloat16 [24576, 8, 128], P(('dp', 'cp')), parts along dimension 0
- value_cache: bfloat16 [24576, 8, 128], P(('dp', 'cp')), parts along dimension 0
- prefix_len: int32 [2], P('dp'), parts along dimension 0
Outputs:
- output 1: bfloat16 [128, 128, 128], P(('dp', 'cp')), parts along dimension 0
- output 2: float32 [128, 128], P(('dp', 'cp')), parts along dimension 0
There are 2 independent parts. A program takes and returns all parts, laid end to end along the dimension named above; each array names one.
All inputs are finite; a program needn't handle non-finite values.
Results may differ from a plain program's by a relative error of at most 0.00879912.
Values are sent between devices in bfloat16 or wider.
A program may use at most 1 GiB of HBM per device.

v0:
```python
import jax
import jax.numpy as jnp
from jax import lax
from jax.sharding import PartitionSpec as P

MASK_FILL = -1e30


def solution(mesh):
    groups = mesh.shape['cp']
    send_pairs = [(src_idx, (src_idx + 1) % groups) for src_idx in range(groups)]
    tok_spec = P(('dp', 'cp'))

    def local_attend(queries, key_new, value_new, key_cache, value_cache, prefix_len):
        tok_rows, num_heads, head_dim = queries.shape
        cache_len, kv_heads = key_cache.shape[0], key_cache.shape[1]
        group_ratio = num_heads // kv_heads
        logit_scale = head_dim ** -0.5
        my_rank = lax.axis_index('cp')
        cache_seen = my_rank * cache_len + jnp.arange(cache_len) < prefix_len[0]
        row_ids = jnp.arange(tok_rows)
        key_ids = my_rank * tok_rows + row_ids

        def absorb(loop_step, q_blk, out_acc, row_max, row_sum):
            source = (my_rank - loop_step) % groups
            q_grouped = q_blk.reshape(tok_rows, kv_heads, group_ratio, head_dim)
            s_cache = jnp.einsum('tkgd,skd->kgts', q_grouped, key_cache, preferred_element_type=jnp.float32) * logit_scale
            s_cache = jnp.where(cache_seen, s_cache, MASK_FILL)
            s_fresh = jnp.einsum('tkgd,skd->kgts', q_grouped, key_new, preferred_element_type=jnp.float32) * logit_scale
            fresh_seen = key_ids[None, :] <= (source * tok_rows + row_ids)[:, None]
            s_fresh = jnp.where(fresh_seen, s_fresh, MASK_FILL)
            next_max = jnp.maximum(row_max, jnp.maximum(s_cache.max(axis=-1), s_fresh.max(axis=-1)))
            e_cache = jnp.exp(s_cache - next_max[..., None])
            e_fresh = jnp.exp(s_fresh - next_max[..., None])
            rescale_by = jnp.exp(row_max - next_max)
            row_sum = row_sum * rescale_by + e_cache.sum(axis=-1) + e_fresh.sum(axis=-1)
            out_acc = (out_acc * rescale_by[..., None]
                       + jnp.einsum('kgts,skd->kgtd', e_cache.astype(jnp.bfloat16), value_cache, preferred_element_type=jnp.float32)
                       + jnp.einsum('kgts,skd->kgtd', e_fresh.astype(jnp.bfloat16), value_new, preferred_element_type=jnp.float32))
            return out_acc, next_max, row_sum

        def one_step(loop_step, state):
            q_blk, out_acc, row_max, row_sum = state
            out_acc, row_max, row_sum = absorb(loop_step, q_blk, out_acc, row_max, row_sum)
            return lax.ppermute((q_blk, out_acc, row_max, row_sum), 'cp', send_pairs)

        start_acc = jnp.zeros((kv_heads, group_ratio, tok_rows, head_dim), jnp.float32)
        start_max = jnp.full((kv_heads, group_ratio, tok_rows), MASK_FILL, jnp.float32)
        start_sum = jnp.zeros((kv_heads, group_ratio, tok_rows), jnp.float32)
        q_blk, out_acc, row_max, row_sum = lax.fori_loop(0, groups - 1, one_step, (queries, start_acc, start_max, start_sum))
        out_acc, row_max, row_sum = absorb(groups - 1, q_blk, out_acc, row_max, row_sum)
        out_acc, row_max, row_sum = lax.ppermute((out_acc, row_max, row_sum), 'cp', send_pairs)
        attn_out = (out_acc / row_sum[..., None]).transpose(2, 0, 1, 3).reshape(tok_rows, num_heads, head_dim).astype(jnp.bfloat16)
        row_lse = (row_max + jnp.log(row_sum)).transpose(2, 0, 1).reshape(tok_rows, num_heads)
        return attn_out, row_lse

    return jax.shard_map(local_attend, mesh=mesh, in_specs=(tok_spec, tok_spec, tok_spec, tok_spec, tok_spec, P('dp')), out_specs=(tok_spec, tok_spec), check_vma=False)
```

profile of v0, /device:TPU:0, one launch (start us, length us, event | category | flops | bytes accessed | tf_op | source)
XLA Modules:
  0.0 276.4 jit_solution(6416321977709756053)
XLA Ops:
  0.6 1.9 copy.110
  2.5 6.3 %copy.13 = bf16[3072,8,128]{2,0,1:T(8,128)(2,1)} copy(bf16[3072,8,128]{2,1,0:T(8,128)(2,1)} %param.11) | data formatting | bytes 12582912
  9.6 6.3 %copy.15 = bf16[3072,8,128]{2,0,1:T(8,128)(2,1)} copy(bf16[3072,8,128]{2,1,0:T(8,128)(2,1)} %param.12) | data formatting | bytes 12582912
  18.0 196.6 %while.22 = (s32[]{:T(128)}, bf16[16,128,128]{2,1,0:T(8,128)(2,1)}, f32[8,16,16,128]{3,2,1,0:T(8,128)S(1)}, f32[8,16,16]{1,2,0:T(8,128)S(1)}, f32[8,16,16]{1,2,0...) while((s32[]{:T(128)}, bf16[16,128,128]{2,1,0:T(8,128)(2,1)}, ...), condition=%wide.region_5.6_spmd.clone, body=%wide.region_0.5_spmd.clone.sunk | while | flops 3308202240 | bytes 101504216 | solution.py:50
  19.8 1.3 fusion.60
  21.2 13.1 %bitcast_reduce_fusion.3 = (f32[8,16,16]{1,2,0:T(8,128)S(1)}, f32[8,3072,16,16]{1,3,2,0:T(8,128)}) fusion(pred[3072]{0:T(1024)(128)(4,1)S(1)} %add_compare_fusion.3, bf16[16,8,16,128]{3,2,1,0:T(8,128)(2,1)S(1)} %bitcast.84, bf16[3072,8,128]{2,0,1:T(8,128)(2,1)} %get-tuple-element.546), kind=kOutput, calls=%fused_computation.4.clone.1 | convolution fusion | flops 1629485056 | bytes 31992832 | tf_op jit(solution)/shard_map/while/body/eval_jaxpr/tkgd,skd->kgts/dot_general | solution.py:27
  35.1 11.3 %fusion.63 = f32[8,16,16]{1,2,0:T(8,128)S(1)} fusion(f32[8,3072,16,16]{1,3,2,0:T(8,128)} %get-tuple-element.501, f32[8,16,16]{1,2,0:T(8,128)S(1)} %maximum_maximum_fusion.3, pred[3072]{0:T(1024)(128)(4,1)S(1)} %add_compare_fusion.3), kind=kLoop, calls=%fused_computation.7.clone.1 | loop fusion | flops 25163776 | bytes 25185280 | tf_op jit(solution)/shard_map/while/body/eval_jaxpr/reduce_sum | solution.py:36
  46.4 13.6 %fusion.62 = f32[8,16,16,128]{3,1,2,0:T(8,128)} fusion(f32[8,3072,16,16]{1,3,2,0:T(8,128)} %get-tuple-element.501, f32[8,16,16]{1,2,0:T(8,128)S(1)} %maximum_maximum_fusion.3, pred[3072]{0:T(1024)(128)(4,1)S(1)} %add_compare_fusion.3, bf16[3072,8,128]{2,0,1:T(8,128)(2,1)} %get-tuple-element.549), kind=kOutput, calls=%fused_computation.9.clone.1 | convolution fusion | flops 1635778560 | bytes 32517120 | tf_op jit(solution)/shard_map/while/body/eval_jaxpr/kgts,skd->kgtd/dot_general | solution.py:38
  60.2 1.7 convolution_add_fusion.3
  62.8 2.6 collective-permute-start
  65.5 18.1 %collective-permute-done.2 = f32[8,16,16]{1,2,0:T(8,128)S(1)} collective-permute-done((f32[8,16,16]{1,2,0:T(8,128)S(1)}, f32[8,16,16]{1,2,0:T(8,128)S(1)}, u32[]{:S(2)}, u32[]{:S(2)}) %collective-permute-start.2) | collective-permute-done | bytes 8224 | tf_op jit(solution)/shard_map/while/body/eval_jaxpr/ppermute | solution.py:45
  86.0 1.3 fusion.60
  87.4 13.1 %bitcast_reduce_fusion.3 = (f32[8,16,16]{1,2,0:T(8,128)S(1)}, f32[8,3072,16,16]{1,3,2,0:T(8,128)}) fusion(pred[3072]{0:T(1024)(128)(4,1)S(1)} %add_compare_fusion.3, bf16[16,8,16,128]{3,2,1,0:T(8,128)(2,1)S(1)} %bitcast.84, bf16[3072,8,128]{2,0,1:T(8,128)(2,1)} %get-tuple-element.546), kind=kOutput, calls=%fused_computation.4.clone.1 | convolution fusion | flops 1629485056 | bytes 31992832 | tf_op jit(solution)/shard_map/while/body/eval_jaxpr/tkgd,skd->kgts/dot_general | solution.py:27
  101.3 11.3 %fusion.63 = f32[8,16,16]{1,2,0:T(8,128)S(1)} fusion(f32[8,3072,16,16]{1,3,2,0:T(8,128)} %get-tuple-element.501, f32[8,16,16]{1,2,0:T(8,128)S(1)} %maximum_maximum_fusion.3, pred[3072]{0:T(1024)(128)(4,1)S(1)} %add_compare_fusion.3), kind=kLoop, calls=%fused_computation.7.clone.1 | loop fusion | flops 25163776 | bytes 25185280 | tf_op jit(solution)/shard_map/while/body/eval_jaxpr/reduce_sum | solution.py:36
  112.6 13.6 %fusion.62 = f32[8,16,16,128]{3,1,2,0:T(8,128)} fusion(f32[8,3072,16,16]{1,3,2,0:T(8,128)} %get-tuple-element.501, f32[8,16,16]{1,2,0:T(8,128)S(1)} %maximum_maximum_fusion.3, pred[3072]{0:T(1024)(128)(4,1)S(1)} %add_compare_fusion.3, bf16[3072,8,128]{2,0,1:T(8,128)(2,1)} %get-tuple-element.549), kind=kOutput, calls=%fused_computation.9.clone.1 | convolution fusion | flops 1635778560 | bytes 32517120 | tf_op jit(solution)/shard_map/while/body/eval_jaxpr/kgts,skd->kgtd/dot_general | solution.py:38
  126.4 1.7 convolution_add_fusion.3
  128.2 2.4 collective-permute-start
  130.6 18.1 %collective-permute-done.2 = f32[8,16,16]{1,2,0:T(8,128)S(1)} collective-permute-done((f32[8,16,16]{1,2,0:T(8,128)S(1)}, f32[8,16,16]{1,2,0:T(8,128)S(1)}, u32[]{:S(2)}, u32[]{:S(2)}) %collective-permute-start.2) | collective-permute-done | bytes 8224 | tf_op jit(solution)/shard_map/while/body/eval_jaxpr/ppermute | solution.py:45
  151.2 1.3 fusion.60
  152.5 13.1 %bitcast_reduce_fusion.3 = (f32[8,16,16]{1,2,0:T(8,128)S(1)}, f32[8,3072,16,16]{1,3,2,0:T(8,128)}) fusion(pred[3072]{0:T(1024)(128)(4,1)S(1)} %add_compare_fusion.3, bf16[16,8,16,128]{3,2,1,0:T(8,128)(2,1)S(1)} %bitcast.84, bf16[3072,8,128]{2,0,1:T(8,128)(2,1)} %get-tuple-element.546), kind=kOutput, calls=%fused_computation.4.clone.1 | convolution fusion | flops 1629485056 | bytes 31992832 | tf_op jit(solution)/shard_map/while/body/eval_jaxpr/tkgd,skd->kgts/dot_general | solution.py:27
  166.5 11.3 %fusion.63 = f32[8,16,16]{1,2,0:T(8,128)S(1)} fusion(f32[8,3072,16,16]{1,3,2,0:T(8,128)} %get-tuple-element.501, f32[8,16,16]{1,2,0:T(8,128)S(1)} %maximum_maximum_fusion.3, pred[3072]{0:T(1024)(128)(4,1)S(1)} %add_compare_fusion.3), kind=kLoop, calls=%fused_computation.7.clone.1 | loop fusion | flops 25163776 | bytes 25185280 | tf_op jit(solution)/shard_map/while/body/eval_jaxpr/reduce_sum | solution.py:36
  177.8 13.6 %fusion.62 = f32[8,16,16,128]{3,1,2,0:T(8,128)} fusion(f32[8,3072,16,16]{1,3,2,0:T(8,128)} %get-tuple-element.501, f32[8,16,16]{1,2,0:T(8,128)S(1)} %maximum_maximum_fusion.3, pred[3072]{0:T(1024)(128)(4,1)S(1)} %add_compare_fusion.3, bf16[3072,8,128]{2,0,1:T(8,128)(2,1)} %get-tuple-element.549), kind=kOutput, calls=%fused_computation.9.clone.1 | convolution fusion | flops 1635778560 | bytes 32517120 | tf_op jit(solution)/shard_map/while/body/eval_jaxpr/kgts,skd->kgtd/dot_general | solution.py:38
  191.6 1.7 convolution_add_fusion.3
  193.3 2.4 collective-permute-start
  195.8 18.1 %collective-permute-done.2 = f32[8,16,16]{1,2,0:T(8,128)S(1)} collective-permute-done((f32[8,16,16]{1,2,0:T(8,128)S(1)}, f32[8,16,16]{1,2,0:T(8,128)S(1)}, u32[]{:S(2)}, u32[]{:S(2)}) %collective-permute-start.2) | collective-permute-done | bytes 8224 | tf_op jit(solution)/shard_map/while/body/eval_jaxpr/ppermute | solution.py:45
  214.6 2.4 fusion.45
  217.0 13.1 %bitcast_reduce_fusion.1 = (f32[8,16,16]{1,2,0:T(8,128)S(1)}, f32[8,16,16,3072]{3,2,1,0:T(8,128)}) fusion(pred[3072]{0:T(1024)(128)(4,1)S(1)} %copy-done, bf16[3072,8,128,1]{2,1,0,3:T(8,128)(2,1)} %bitcast.85, bf16[16,8,16,128]{3,2,1,0:T(8,128)(2,1)} %bitcast.1), kind=kOutput, calls=%fused_computation.36 | convolution fusion | flops 1629485056 | bytes 31992832 | tf_op jit(solution)/shard_map/tkgd,skd->kgts/dot_general | solution.py:27
  230.9 11.3 %fusion.26 = f32[8,16,16]{1,2,0:T(8,128)S(1)} fusion(f32[8,16,16,3072]{3,2,1,0:T(8,128)} %get-tuple-element.405, f32[8,16,16]{1,2,0:T(8,128)S(1)} %maximum_maximum_fusion.1, pred[3072]{0:T(1024)(128)(4,1)S(1)} %copy-done), kind=kLoop, calls=%fused_computation.39 | loop fusion | flops 25163776 | bytes 25185280 | tf_op jit(solution)/shard_map/reduce_sum | solution.py:36
  242.2 14.6 %fusion.28 = f32[8,16,16,128]{3,1,2,0:T(8,128)} fusion(f32[8,16,16,3072]{3,2,1,0:T(8,128)} %get-tuple-element.405, f32[8,16,16]{1,2,0:T(8,128)S(1)} %maximum_maximum_fusion.1, pred[3072]{0:T(1024)(128)(4,1)S(1)} %copy-done, bf16[3072,8,128,1]{2,1,0,3:T(8,128)(2,1)} %bitcast.86), kind=kOutput, calls=%fused_computation.41 | convolution fusion | flops 1635778560 | bytes 32517120 | tf_op jit(solution)/shard_map/kgts,skd->kgtd/dot_general | solution.py:38
  256.9 1.7 convolution_add_fusion.1
  258.7 2.4 collective-permute-start.5
  261.1 12.5 %collective-permute-done.5 = f32[8,16,16]{1,2,0:T(8,128)S(1)} collective-permute-done((f32[8,16,16]{1,2,0:T(8,128)S(1)}, f32[8,16,16]{1,2,0:T(8,128)S(1)}, u32[]{:S(2)}, u32[]{:S(2)}) %collective-permute-start.5) | collective-permute-done | bytes 8224 | tf_op jit(solution)/shard_map/ppermute | solution.py:52
  (79 shorter events, 17.3 us)
Async XLA Ops:
  0.6 15.3 %copy-start.1 = (bf16[16,8,128]{2,1,0:T(8,128)(2,1)S(1)}, bf16[16,8,128]{2,1,0:T(8,128)(2,1)}, u32[]{:S(2)}) copy-start(bf16[16,8,128]{2,1,0:T(8,128)(2,1)} %param.10) | copy-start | bytes 98308
  18.0 196.6 %copy-start.3 = (pred[16,16]{1,0:T(8,128)(4,1)S(1)}, pred[16,16]{1,0:T(8,128)(4,1)}, u32[]{:S(2)}) copy-start(pred[16,16]{1,0:T(8,128)(4,1)} %broadcast_compare_fusion.1) | copy-start | bytes 772
  18.0 199.0 %copy-start = (pred[3072]{0:T(1024)(128)(4,1)S(1)}, pred[3072]{0:T(1024)(128)(4,1)}, u32[]{:S(2)}) copy-start(pred[3072]{0:T(1024)(128)(4,1)} %add_compare_fusion.1) | copy-start | bytes 9220
  61.9 22.3 %collective-permute-start.1 = (f32[8,16,16,128]{3,2,1,0:T(8,128)S(1)}, f32[8,16,16,128]{3,2,1,0:T(8,128)S(1)}, u32[]{:S(2)}, u32[]{:S(2)}) collective-permute-start(f32[8,16,16,128]{3,2,1,0:T(8,128)S(1)} %convolution_add_fusion.3), channel_id=1, source_target_pairs={{0,1},{1,2},{2,3},{3,0},{4,5},{5,6},{6,7},{7,4}} | collective-permute-start | bytes 3145736 | tf_op jit(solution)/shard_map/while/body/eval_jaxpr/ppermute | solution.py:45
  62.8 21.4 %collective-permute-start = (bf16[16,128,128]{2,1,0:T(8,128)(2,1)S(1)}, bf16[16,128,128]{2,1,0:T(8,128)(2,1)}, u32[]{:S(2)}, u32[]{:S(2)}) collective-permute-start(bf16[16,128,128]{2,1,0:T(8,128)(2,1)S(1)} %copy.99), channel_id=1, source_target_pairs={{0,1},{1,2},{2,3},{3,0},{4,5},{5,6},{6,7},{7,4}} | collective-permute-start | bytes 1572872 | tf_op jit(solution)/shard_map/while/body/eval_jaxpr/ppermute | solution.py:45
  65.4 18.1 %collective-permute-start.2 = (f32[8,16,16]{1,2,0:T(8,128)S(1)}, f32[8,16,16]{1,2,0:T(8,128)S(1)}, u32[]{:S(2)}, u32[]{:S(2)}) collective-permute-start(f32[8,16,16]{1,2,0:T(8,128)S(1)} %maximum_maximum_fusion.3), channel_id=1, source_target_pairs={{0,1},{1,2},{2,3},{3,0},{4,5},{5,6},{6,7},{7,4}} | collective-permute-start | bytes 24584 | tf_op jit(solution)/shard_map/while/body/eval_jaxpr/ppermute | solution.py:45
  65.4 18.8 %collective-permute-start.3 = (f32[8,16,16]{1,2,0:T(8,128)S(1)}, f32[8,16,16]{1,2,0:T(8,128)S(1)}, u32[]{:S(2)}, u32[]{:S(2)}) collective-permute-start(f32[8,16,16]{1,2,0:T(8,128)S(1)} %get-tuple-element.504), channel_id=1, source_target_pairs={{0,1},{1,2},{2,3},{3,0},{4,5},{5,6},{6,7},{7,4}} | collective-permute-start | bytes 24584 | tf_op jit(solution)/shard_map/while/body/eval_jaxpr/ppermute | solution.py:45
  128.1 21.3 %collective-permute-start.1 = (f32[8,16,16,128]{3,2,1,0:T(8,128)S(1)}, f32[8,16,16,128]{3,2,1,0:T(8,128)S(1)}, u32[]{:S(2)}, u32[]{:S(2)}) collective-permute-start(f32[8,16,16,128]{3,2,1,0:T(8,128)S(1)} %convolution_add_fusion.3), channel_id=1, source_target_pairs={{0,1},{1,2},{2,3},{3,0},{4,5},{5,6},{6,7},{7,4}} | collective-permute-start | bytes 3145736 | tf_op jit(solution)/shard_map/while/body/eval_jaxpr/ppermute | solution.py:45
  128.2 21.2 %collective-permute-start = (bf16[16,128,128]{2,1,0:T(8,128)(2,1)S(1)}, bf16[16,128,128]{2,1,0:T(8,128)(2,1)}, u32[]{:S(2)}, u32[]{:S(2)}) collective-permute-start(bf16[16,128,128]{2,1,0:T(8,128)(2,1)S(1)} %copy.99), channel_id=1, source_target_pairs={{0,1},{1,2},{2,3},{3,0},{4,5},{5,6},{6,7},{7,4}} | collective-permute-start | bytes 1572872 | tf_op jit(solution)/shard_map/while/body/eval_jaxpr/ppermute | solution.py:45
  130.6 18.1 %collective-permute-start.2 = (f32[8,16,16]{1,2,0:T(8,128)S(1)}, f32[8,16,16]{1,2,0:T(8,128)S(1)}, u32[]{:S(2)}, u32[]{:S(2)}) collective-permute-start(f32[8,16,16]{1,2,0:T(8,128)S(1)} %maximum_maximum_fusion.3), channel_id=1, source_target_pairs={{0,1},{1,2},{2,3},{3,0},{4,5},{5,6},{6,7},{7,4}} | collective-permute-start | bytes 24584 | tf_op jit(solution)/shard_map/while/body/eval_jaxpr/ppermute | solution.py:45
  130.6 18.8 %collective-permute-start.3 = (f32[8,16,16]{1,2,0:T(8,128)S(1)}, f32[8,16,16]{1,2,0:T(8,128)S(1)}, u32[]{:S(2)}, u32[]{:S(2)}) collective-permute-start(f32[8,16,16]{1,2,0:T(8,128)S(1)} %get-tuple-element.504), channel_id=1, source_target_pairs={{0,1},{1,2},{2,3},{3,0},{4,5},{5,6},{6,7},{7,4}} | collective-permute-start | bytes 24584 | tf_op jit(solution)/shard_map/while/body/eval_jaxpr/ppermute | solution.py:45
  193.3 21.3 %collective-permute-start.1 = (f32[8,16,16,128]{3,2,1,0:T(8,128)S(1)}, f32[8,16,16,128]{3,2,1,0:T(8,128)S(1)}, u32[]{:S(2)}, u32[]{:S(2)}) collective-permute-start(f32[8,16,16,128]{3,2,1,0:T(8,128)S(1)} %convolution_add_fusion.3), channel_id=1, source_target_pairs={{0,1},{1,2},{2,3},{3,0},{4,5},{5,6},{6,7},{7,4}} | collective-permute-start | bytes 3145736 | tf_op jit(solution)/shard_map/while/body/eval_jaxpr/ppermute | solution.py:45
  193.3 21.2 %collective-permute-start = (bf16[16,128,128]{2,1,0:T(8,128)(2,1)S(1)}, bf16[16,128,128]{2,1,0:T(8,128)(2,1)}, u32[]{:S(2)}, u32[]{:S(2)}) collective-permute-start(bf16[16,128,128]{2,1,0:T(8,128)(2,1)S(1)} %copy.99), channel_id=1, source_target_pairs={{0,1},{1,2},{2,3},{3,0},{4,5},{5,6},{6,7},{7,4}} | collective-permute-start | bytes 1572872 | tf_op jit(solution)/shard_map/while/body/eval_jaxpr/ppermute | solution.py:45
  195.7 18.1 %collective-permute-start.2 = (f32[8,16,16]{1,2,0:T(8,128)S(1)}, f32[8,16,16]{1,2,0:T(8,128)S(1)}, u32[]{:S(2)}, u32[]{:S(2)}) collective-permute-start(f32[8,16,16]{1,2,0:T(8,128)S(1)} %maximum_maximum_fusion.3), channel_id=1, source_target_pairs={{0,1},{1,2},{2,3},{3,0},{4,5},{5,6},{6,7},{7,4}} | collective-permute-start | bytes 24584 | tf_op jit(solution)/shard_map/while/body/eval_jaxpr/ppermute | solution.py:45
  195.8 18.8 %collective-permute-start.3 = (f32[8,16,16]{1,2,0:T(8,128)S(1)}, f32[8,16,16]{1,2,0:T(8,128)S(1)}, u32[]{:S(2)}, u32[]{:S(2)}) collective-permute-start(f32[8,16,16]{1,2,0:T(8,128)S(1)} %get-tuple-element.504), channel_id=1, source_target_pairs={{0,1},{1,2},{2,3},{3,0},{4,5},{5,6},{6,7},{7,4}} | collective-permute-start | bytes 24584 | tf_op jit(solution)/shard_map/while/body/eval_jaxpr/ppermute | solution.py:45
  242.2 14.7 %copy-start.2 = (bf16[16,8,128]{2,1,0:T(8,128)(2,1)S(1)}, bf16[16,8,128]{2,1,0:T(8,128)(2,1)}, u32[]{:S(2)}) copy-start(bf16[16,8,128]{2,1,0:T(8,128)(2,1)} %param.10) | copy-start | bytes 98308
  258.7 16.5 %collective-permute-start.4 = (f32[8,16,16,128]{3,2,1,0:T(8,128)S(1)}, f32[8,16,16,128]{3,2,1,0:T(8,128)S(1)}, u32[]{:S(2)}, u32[]{:S(2)}) collective-permute-start(f32[8,16,16,128]{3,2,1,0:T(8,128)S(1)} %convolution_add_fusion.1), channel_id=1, source_target_pairs={{0,1},{1,2},{2,3},{3,0},{4,5},{5,6},{6,7},{7,4}} | collective-permute-start | bytes 3145736 | tf_op jit(solution)/shard_map/ppermute | solution.py:52
  258.7 14.9 %collective-permute-start.5 = (f32[8,16,16]{1,2,0:T(8,128)S(1)}, f32[8,16,16]{1,2,0:T(8,128)S(1)}, u32[]{:S(2)}, u32[]{:S(2)}) collective-permute-start(f32[8,16,16]{1,2,0:T(8,128)S(1)} %get-tuple-element.394), channel_id=1, source_target_pairs={{0,1},{1,2},{2,3},{3,0},{4,5},{5,6},{6,7},{7,4}} | collective-permute-start | bytes 24584 | tf_op jit(solution)/shard_map/ppermute | solution.py:52
  261.1 13.2 %collective-permute-start.6 = (f32[8,16,16]{1,2,0:T(8,128)S(1)}, f32[8,16,16]{1,2,0:T(8,128)S(1)}, u32[]{:S(2)}, u32[]{:S(2)}) collective-permute-start(f32[8,16,16]{1,2,0:T(8,128)S(1)} %maximum_maximum_fusion.1), channel_id=1, source_target_pairs={{0,1},{1,2},{2,3},{3,0},{4,5},{5,6},{6,7},{7,4}} | collective-permute-start | bytes 24584 | tf_op jit(solution)/shard_map/ppermute | solution.py:52
where the time goes:
time: 277 us; the launch traced here: 276 us
  matrix products  121 us (44%)
  waiting for transfers between devices  69.5 us (25%)
  other arithmetic  50.6 us (18%)
  local copies, waits for them, and re-layouts  22.4 us (8%)
  starting transfers between devices  11 us (4%)
    ppermute x12, waiting for transfers between devices, one_step(): return lax.ppermute((q_blk, out_acc, row_max, row_sum), 'cp', send_pairs)  56.3 us
    dot_general x4, matrix products, absorb(): jnp.einsum('kgts,skd->kgtd', e_cache.astype(jnp.bfloat16), value_cache, p...  55.5 us
    dot_general x4, matrix products, absorb(): jnp.einsum('tkgd,skd->kgts', q_grouped, key_cache, preferred_element_type...  52.4 us
    reduce_sum x8, other arithmetic, absorb(): row_sum = row_sum * rescale_by + e_cache.sum(axis=-1) + e_fresh.sum(axis=-1)  46.6 us
    unnamed x14, local copies, waits for them, and re-layouts  16.2 us
    ppermute x3, waiting for transfers between devices, local_attend(): lax.ppermute((out_acc, row_max, row_sum), 'cp', send_pairs)  13.2 us
    ppermute x12, starting transfers between devices, one_step(): return lax.ppermute((q_blk, out_acc, row_max, row_sum), 'cp', send_pairs)  8.58 us
    dot_general x4, matrix products, absorb(): jnp.einsum('kgts,skd->kgtd', e_fresh.astype(jnp.bfloat16), value_new, pre...  6.94 us
  transfers between devices with their start and end apart: 15, of which 8 were waited for; matrix products, arithmetic and copies ran while one was open for 0% of the time, Pallas kernels for 0%

commit v1 on v0

v1 whole, which is shorter than its diff:
```python
import functools
import math

import jax
import jax.numpy as jnp
from jax import lax
from jax.experimental import pallas as pl
from jax.experimental.pallas import tpu as pltpu
from jax.sharding import PartitionSpec as P

MESH = pl.DeviceIdType.MESH
BIG = 1e30
TK = 256
PREP = 128
BF = jnp.bfloat16
F32 = jnp.float32


def attend_kernel(q_hbm, kn_hbm, vn_hbm, kc_hbm, vc_hbm, plen_ref, out_hbm, lse_hbm,
                  raw_k, raw_v, new_k, new_v, kbuf, vbuf, bias, qraw, qt, s0, s1, m0, m1,
                  st_o, st_m, st_l, ps, psl, pr, prl, fo, fl,
                  raw_sem, new_sem, q_send, q_recv, kv_send, k_recv, v_recv, p_send, p_recv, f_send, f_recv):
    tok, kvh, ratio, dim = q_hbm.shape
    cache = kc_hbm.shape[0] // kvh
    half = kvh // 2
    rows = tok * ratio
    n_raw = raw_sem.shape[1]
    raw_pos = cache // n_raw
    chunks = cache // TK
    scale2 = dim ** -0.5 * math.log2(math.e)

    me = lax.axis_index('cp')
    core = lax.rem(me, 2)
    chip2 = me - core
    mate = chip2 + 1 - core
    far = lax.rem(chip2 + 2, 4) + core
    far_other = lax.rem(chip2 + 2, 4) + 1 - core

    def raw_copy(j):
        sl = pl.ds(j * raw_pos * kvh, raw_pos * kvh)
        return (pltpu.make_async_copy(kc_hbm.at[sl], raw_k.at[sl], raw_sem.at[0, j]),
                pltpu.make_async_copy(vc_hbm.at[sl], raw_v.at[sl], raw_sem.at[1, j]))

    def own_q(h):
        return pltpu.make_async_copy(q_hbm.at[:, half * core + h], qraw.at[h], q_recv.at[h])

    for j in range(n_raw):
        a, b = raw_copy(j)
        a.start()
        b.start()
    new_copies = (pltpu.make_async_copy(kn_hbm, new_k, new_sem.at[0]),
                  pltpu.make_async_copy(vn_hbm, new_v, new_sem.at[1]))
    for cp in new_copies:
        cp.start()
    for h in range(half):
        own_q(h).start()

    barrier = pltpu.get_barrier_semaphore()
    for peer in (mate, far, far_other):
        pl.semaphore_signal(barrier, inc=1, device_id={'cp': peer}, device_id_type=MESH)

    ones_row = jnp.where(lax.broadcasted_iota(jnp.int32, (dim, rows), 0) == 0, 1.0, 0.0).astype(BF)

    @pl.loop(0, 4 * half)
    def _(j):
        qt[j, pl.ds(dim, dim), :] = ones_row
        st_o[j] = jnp.zeros((dim, rows), F32)
        st_m[j] = jnp.full((1, rows), -1e38, F32)
        st_l[j] = jnp.zeros((1, rows), F32)

    pl.semaphore_wait(barrier, 3)

    def q_copy(k, h):
        peer, base = ((far, 2 * half), (far_other, 3 * half), (mate, half))[k]
        peer_core = (core, 1 - core, 1 - core)[k]
        return pltpu.make_async_remote_copy(
            src_ref=q_hbm.at[:, half * peer_core + h], dst_ref=qraw.at[base + h],
            send_sem=q_send.at[k * half + h], recv_sem=q_recv.at[base + h],
            device_id={'cp': peer}, device_id_type=MESH)

    for k in range(3):
        for h in range(half):
            q_copy(k, h).start()

    visible_len = plen_ref[0]
    for f, owner in enumerate((me, mate)):
        @pl.loop(0, chunks)
        def _(j):
            lane = lax.broadcasted_iota(jnp.int32, (TK, dim), 1)
            pos = owner * cache + j * TK + lax.broadcasted_iota(jnp.int32, (TK, dim), 0)
            hidden = jnp.logical_and(lane == 0, pos >= visible_len)
            bias[f, pl.ds(pl.multiple_of(j * TK, TK), TK), :] = jnp.where(hidden, -BIG, 0.0).astype(BF)

    for cp in new_copies:
        cp.wait()
    kt = pltpu.einshape('phd->hpd', new_k[...].reshape(tok, kvh, dim))
    vt = pltpu.einshape('phd->hpd', new_v[...].reshape(tok, kvh, dim))
    for h in range(kvh):
        kbuf[h, pl.ds(cache, tok), :] = kt[h]
        vpad = jnp.concatenate([vt[h].astype(F32), jnp.zeros((dim - tok, dim), F32)], axis=0)
        vbuf[h, :, pl.ds(cache, dim)] = vpad.T.astype(BF)
    for j in range(n_raw):
        for cp in raw_copy(j):
            cp.wait()

        @pl.loop(0, raw_pos // PREP)
        def _(i):
            base = pl.multiple_of(j * raw_pos + i * PREP, PREP)
            src = pl.ds(pl.multiple_of(base * kvh, PREP * kvh), PREP * kvh)
            xk = pltpu.einshape('phd->hpd', raw_k[src, :].reshape(PREP, kvh, dim))
            xv = pltpu.einshape('phd->hpd', raw_v[src, :].reshape(PREP, kvh, dim))
            for h in range(kvh):
                kbuf[h, pl.ds(base, PREP), :] = xk[h]
                vbuf[h, :, pl.ds(base, PREP)] = xv[h].T

    def kv_copies(h):
        src = half * (1 - core) + h
        return tuple(
            pltpu.make_async_remote_copy(
                src_ref=buf.at[src], dst_ref=buf.at[kvh + h], send_sem=kv_send.at[w, h], recv_sem=recv.at[h],
                device_id={'cp': mate}, device_id_type=MESH)
            for w, (buf, recv) in enumerate(((kbuf, k_recv), (vbuf, v_recv))))

    for h in range(half):
        for cp in kv_copies(h):
            cp.start()

    def item(s):
        second = lax.div(s, 4 * half)
        slot = lax.rem(s + second * 2 * half, 4 * half)
        h = lax.rem(slot, half)
        kv = jnp.where(second == 1, kvh + h, half * core + h)
        owner = jnp.where(second == 1, mate, me)
        src = lax.div(slot, half)
        home = jnp.where(src == 0, me, jnp.where(src == 1, mate, jnp.where(src == 2, far, far_other)))
        return second, slot, kv, owner, home

    def load_q(slot):
        qt[slot, pl.ds(0, dim), :] = qraw[slot].reshape(rows, dim).T

    def qk_tile(kv, f, c, qv):
        sl = pl.ds(c * TK, TK)
        lhs = jnp.concatenate([kbuf[kv, sl, :], bias[f, sl, :]], axis=1)
        return jnp.dot(lhs, qv, preferred_element_type=F32)

    def qk_new(kv, owner, home, qv):
        lhs = jnp.concatenate([kbuf[kv, pl.ds(cache, tok), :], jnp.zeros((tok, dim), BF)], axis=1)
        st = jnp.dot(lhs, qv, preferred_element_type=F32)
        key = owner * tok + lax.broadcasted_iota(jnp.int32, (tok, rows), 0)
        query = home * tok + lax.broadcasted_iota(jnp.int32, (tok, rows), 1) // ratio
        return jnp.where(key <= query, st, -BIG)

    def fold_max(mx, st):
        t = jnp.max(st.reshape(st.shape[0] // 8, 8, rows), axis=0)
        return t if mx is None else jnp.maximum(mx, t)

    def first_scores():
        f, slot, kv, owner, home = item(0)
        qv = qt[slot]
        mx = None
        for c in range(chunks):
            st = qk_tile(kv, f, c, qv)
            s0[pl.ds(c * TK, TK), :] = st
            mx = fold_max(mx, st)
        st = qk_new(kv, owner, home, qv)
        s0[pl.ds(cache, tok), :] = st
        m0[...] = fold_max(mx, st)

    def step(s, sc, sn, mc, mn):
        nxt = lax.rem(s + 1, 8 * half)
        f_n, slot_n, kv_n, owner_n, home_n = item(nxt)
        _, slot, kv, _, _ = item(s)

        ahead = s + 2

        @pl.when(jnp.logical_and(ahead >= half, ahead < 4 * half))
        def _():
            pltpu.make_async_copy(qraw.at[ahead], qraw.at[ahead], q_recv.at[ahead]).wait()

        @pl.when(jnp.logical_and(nxt >= 4 * half, nxt < 5 * half))
        def _():
            h = nxt - 4 * half
            pltpu.make_async_copy(kbuf.at[kvh + h], kbuf.at[kvh + h], k_recv.at[h]).wait()
            pltpu.make_async_copy(vbuf.at[kvh + h], vbuf.at[kvh + h], v_recv.at[h]).wait()

        qv = qt[slot_n]
        m_old = st_m[slot]
        m = jnp.maximum(m_old, jnp.max(mc[...], axis=0, keepdims=True) * scale2)
        decay = jnp.exp2(m_old - m)
        mx = None
        l8 = jnp.zeros((8, rows), F32)
        o = None
        for c in range(chunks):
            sl = pl.ds(c * TK, TK)
            st = qk_tile(kv_n, f_n, c, qv)
            p = jnp.exp2(sc[sl, :] * scale2 - m)
            sn[sl, :] = st
            mx = fold_max(mx, st)
            l8 = l8 + jnp.sum(p.reshape(TK // 8, 8, rows), axis=0)
            t = jnp.dot(vbuf[kv, :, sl], p.astype(BF), preferred_element_type=F32)
            o = t if o is None else o + t
        st = qk_new(kv_n, owner_n, home_n, qv)
        sl = pl.ds(cache, tok)
        p = jnp.exp2(sc[sl, :] * scale2 - m)
        sn[sl, :] = st
        mn[...] = fold_max(mx, st)
        l8 = l8 + jnp.sum(p.reshape(tok // 8, 8, rows), axis=0)
        pb = jnp.concatenate([p.astype(BF), jnp.zeros((dim - tok, rows), BF)], axis=0)
        o = o + jnp.dot(vbuf[kv, :, pl.ds(cache, dim)], pb, preferred_element_type=F32)
        st_o[slot] = st_o[slot] * decay + o
        st_l[slot] = st_l[slot] * decay + jnp.sum(l8, axis=0, keepdims=True)
        st_m[slot] = m
        load_q(jnp.minimum(ahead, 4 * half - 1))

    def partial_copies(u):
        return (pltpu.make_async_remote_copy(
                    src_ref=ps.at[u], dst_ref=pr.at[u], send_sem=p_send.at[0, u], recv_sem=p_recv.at[0, u],
                    device_id={'cp': far}, device_id_type=MESH),
                pltpu.make_async_remote_copy(
                    src_ref=psl.at[u], dst_ref=prl.at[u], send_sem=p_send.at[1, u], recv_sem=p_recv.at[1, u],
                    device_id={'cp': far}, device_id_type=MESH))

    def own_out(u):
        hh = half * core + u
        return (pltpu.make_async_copy(fo.at[u], out_hbm.at[:, hh], f_send.at[0, u]),
                pltpu.make_async_copy(fl.at[u], lse_hbm.at[hh], f_send.at[1, u]))

    def mate_out(u):
        hh = half * core + u - half
        return (pltpu.make_async_remote_copy(
                    src_ref=fo.at[u], dst_ref=out_hbm.at[:, hh], send_sem=f_send.at[0, u],
                    recv_sem=f_recv.at[0, u - half], device_id={'cp': mate}, device_id_type=MESH),
                pltpu.make_async_remote_copy(
                    src_ref=fl.at[u], dst_ref=lse_hbm.at[hh], send_sem=f_send.at[1, u],
                    recv_sem=f_recv.at[1, u - half], device_id={'cp': mate}, device_id_type=MESH))

    def finish(s):
        @pl.when(jnp.logical_and(s >= 4 * half, s < 6 * half))
        def _():
            u = s - 4 * half
            slot = u + 2 * half
            l = st_l[slot]
            ps[u] = (st_o[slot] * (1.0 / l)).astype(BF)
            psl[u] = st_m[slot] + jnp.log2(l)
            for cp in partial_copies(u):
                cp.start()

        @pl.when(s >= 6 * half)
        def _():
            u = s - 6 * half
            for cp in partial_copies(u):
                cp.wait_recv()
            m_a, m_b = st_m[u], prl[u]
            m = jnp.maximum(m_a, m_b)
            a, b = jnp.exp2(m_a - m), jnp.exp2(m_b - m)
            l = st_l[u] * a + b
            inv = 1.0 / l
            o = st_o[u] * (a * inv) + pr[u].astype(F32) * (b * inv)
            fo[u] = o.T.astype(BF).reshape(tok, ratio, dim)
            fl[u] = (m + jnp.log2(l)) * math.log(2.0)

            @pl.when(u < half)
            def _():
                for cp in own_out(u):
                    cp.start()

            @pl.when(u >= half)
            def _():
                for cp in mate_out(u):
                    cp.start()

    for h in range(half):
        own_q(h).wait()
    load_q(0)
    load_q(1)
    first_scores()

    @pl.loop(0, 4 * half)
    def _(i):
        step(2 * i, s0, s1, m0, m1)
        finish(2 * i)
        step(2 * i + 1, s1, s0, m1, m0)
        finish(2 * i + 1)

    for k in range(3):
        for h in range(half):
            q_copy(k, h).wait_send()
    for h in range(half):
        for cp in kv_copies(h):
            cp.wait_send()
    for u in range(2 * half):
        for cp in partial_copies(u):
            cp.wait_send()
    for u in range(half):
        for cp in own_out(u):
            cp.wait()
        for cp in mate_out(u + half):
            cp.wait_send()
            cp.wait_recv()


def solution(mesh):
    tok_spec = P(('dp', 'cp'))

    def local(queries, key_new, value_new, key_cache, value_cache, prefix_len):
        tok, heads, dim = queries.shape
        cache, kvh = key_cache.shape[:2]
        ratio = heads // kvh
        half = kvh // 2
        rows = tok * ratio
        n_raw = 6
        dma = pltpu.SemaphoreType.DMA
        hbm = pl.BlockSpec(memory_space=pl.ANY)
        scratch = [
            pltpu.VMEM((cache * kvh, dim), BF),
            pltpu.VMEM((cache * kvh, dim), BF),
            pltpu.VMEM((tok * kvh, dim), BF),
            pltpu.VMEM((tok * kvh, dim), BF),
            pltpu.VMEM((kvh + half, cache + tok, dim), BF),
            pltpu.VMEM((kvh + half, dim, cache + dim), BF),
            pltpu.VMEM((2, cache, dim), BF),
            pltpu.VMEM((4 * half, tok, ratio, dim), BF),
            pltpu.VMEM((4 * half, 2 * dim, rows), BF),
            pltpu.VMEM((cache + tok, rows), F32),
            pltpu.VMEM((cache + tok, rows), F32),
            pltpu.VMEM((8, rows), F32),
            pltpu.VMEM((8, rows), F32),
            pltpu.VMEM((4 * half, dim, rows), F32),
            pltpu.VMEM((4 * half, 1, rows), F32),
            pltpu.VMEM((4 * half, 1, rows), F32),
            pltpu.VMEM((2 * half, dim, rows), BF),
            pltpu.VMEM((2 * half, 1, rows), F32),
            pltpu.VMEM((2 * half, dim, rows), BF),
            pltpu.VMEM((2 * half, 1, rows), F32),
            pltpu.VMEM((2 * half, tok, ratio, dim), BF),
            pltpu.VMEM((2 * half, 1, rows), F32),
            dma((2, n_raw)), dma((2,)), dma((3 * half,)), dma((4 * half,)), dma((2, half)), dma((half,)), dma((half,)),
            dma((2, 2 * half)), dma((2, 2 * half)), dma((2, 2 * half)), dma((2, half)),
        ]
        flops = 4 * heads * tok * 4 * cache * dim
        out, lse = pl.pallas_call(
            attend_kernel,
            out_shape=(jax.ShapeDtypeStruct((tok, kvh, ratio, dim), BF), jax.ShapeDtypeStruct((kvh, 1, rows), F32)),
            in_specs=[hbm] * 5 + [pl.BlockSpec(memory_space=pltpu.SMEM)],
            out_specs=(hbm, hbm),
            scratch_shapes=scratch,
            compiler_params=pltpu.CompilerParams(collective_id=0, has_side_effects=True, vmem_limit_bytes=63 * 2 ** 20),
            cost_estimate=pl.CostEstimate(flops=flops, bytes_accessed=4 * cache * kvh * dim, transcendentals=heads * tok * 4 * cache),
            name='attend',
        )(queries.reshape(tok, kvh, ratio, dim), key_new.reshape(tok * kvh, dim), value_new.reshape(tok * kvh, dim),
          key_cache.reshape(cache * kvh, dim), value_cache.reshape(cache * kvh, dim), prefix_len)
        row_lse = lse.reshape(kvh, tok, ratio).transpose(1, 0, 2).reshape(tok, heads)
        return out.reshape(tok, heads, dim), row_lse

    return jax.shard_map(local, mesh=mesh, in_specs=(tok_spec, tok_spec, tok_spec, tok_spec, tok_spec, P('dp')),
                         out_specs=(tok_spec, tok_spec), check_vma=False)
```

time: 277 us -> 50.2 us (0.18)
  matrix products: 121 us -> 0 us
  waiting for transfers between devices: 69.5 us -> 0 us
  other arithmetic: 50.6 us -> 0.72 us
  Pallas kernels: 0 us -> 45.3 us
  local copies, waits for them, and re-layouts: 22.4 us -> 2.66 us
  starting transfers between devices: 11 us -> 0 us
    dot_general x16 -> x0, matrix products: 121 us -> none  [the longest x4 55.5 us: absorb(): jnp.einsum('kgts,skd->kgtd', e_cache.astype(jnp.bfloat16), value_cache, p...]
    ppermute x15 -> x0, waiting for transfers between devices: 69.5 us -> none  [the longest x12 56.3 us: one_step(): return lax.ppermute((q_blk, out_acc, row_max, row_sum), 'cp', send_pairs)]
    reduce_sum x8 -> x0, other arithmetic: 46.6 us -> none  [absorb(): row_sum = row_sum * rescale_by + e_cache.sum(axis=-1) + e_fresh.sum(axis=-1)]
    pallas_call x0 -> x1, Pallas kernels: none -> 45.3 us  [local(): pl.pallas_call(attend_kernel, out_shape=(jax.ShapeDtypeStruct((tok, kvh,...]
    unnamed x14 -> x1, local copies, waits for them, and re-layouts: 16.2 us -> 1.88 us
    ppermute x15 -> x0, starting transfers between devices: 11 us -> none  [the longest x12 8.58 us: one_step(): return lax.ppermute((q_blk, out_acc, row_max, row_sum), 'cp', send_pairs)]
    while x3 -> x0, local copies, waits for them, and re-layouts: 3.13 us -> none
  transfers between devices with their start and end apart: 15 -> 0, of which waited for: 8 -> 0; matrix products, arithmetic and copies ran while one was open for 0% -> 0% of each run, Pallas kernels for 0% -> 0%
where the time goes in v1:
time: 50.2 us; the launch traced here: 50 us
  Pallas kernels  45.3 us (90%)
  local copies, waits for them, and re-layouts  2.66 us (5%)
  between operations  1.3 us (3%)
  other arithmetic  0.72 us (1%)
    pallas_call x1, Pallas kernels, local(): pl.pallas_call(attend_kernel, out_shape=(jax.ShapeDtypeStruct((tok, kvh,...  45.3 us
    unnamed x1, local copies, waits for them, and re-layouts  1.88 us

profile of v1, /device:TPU:0, one launch (start us, length us, event | category | flops | bytes accessed | tf_op | source)
XLA Modules:
  0.0 50.0 jit_solution(7368024634714683904)
XLA Ops:
  1.3 45.3 %attend.1 = (bf16[16,8,16,128]{3,2,1,0:T(8,128)(2,1)}, f32[8,1,256]{2,1,0:T(1,128)}) custom-call(bf16[16,8,16,128]{3,2,1,0:T(8,128)(2,1)} %bitcast.11, bf16[128,128]{1,0:T(8,128)(2,1)} %bitcast.12, bf16[128,128]{1,0:T(8,128)(2,1)} %bitcast.13, bf16[24576,128]{1,0:T(8,128)(2,1)} %bitcast.9, bf16[24576,128]{1,0:T(8,128)(2,1)} %bitcast.10, s32[1]{0:T(128)S(6)} %copy.10.plen_ref), custom_call_target="tpu_custom_call" | custom-call | flops 12884901888 | bytes 12582912 | tf_op jit(solution)/shard_map/attend/pallas_call | solution.py:341
  46.6 0.7 %reduce = f32[8,256]{1,0:T(8,128)S(1)} reduce(f32[8,1,256]{2,1,0:T(1,128)} %get-tuple-element.5, f32[]{:T(128)} %constant.1), dimensions={1}, to_apply=%get-tuple-element.5.reduce_sub_computation | reduce | bytes 16388 | tf_op jit(solution)/shard_map/attend/pallas_call | solution.py:341
  47.3 0.1 reshape.34
  47.4 0.7 %reshape.35 = f32[16,128]{1,0:T(8,128)} reshape(f32[16,8,16]{2,1,0:T(8,128)S(1)} %copy.8) | data formatting | bytes 16384 | tf_op jit(solution)/shard_map/reshape | solution.py:352
  48.1 1.9 %copy.11 = bf16[16,128,128]{2,1,0:T(8,128)(2,1)} copy(bf16[16,128,128]{2,1,0:T(8,128)(2,1)} %bitcast.7) | data formatting | bytes 1048576
  (1 shorter events, 0.0 us)

commit v2 on v1

--- a/solution.py
+++ b/solution.py
@@ -17,7 +17,7 @@
 
 
 def attend_kernel(q_hbm, kn_hbm, vn_hbm, kc_hbm, vc_hbm, plen_ref, out_hbm, lse_hbm,
-                  raw_k, raw_v, new_k, new_v, kbuf, vbuf, bias, qraw, qt, s0, s1, m0, m1,
+                  raw_k, raw_v, new_k, new_v, kbuf, vbuf, bias, qraw, qt, s_even, s_odd, m_even, m_odd,
                   st_o, st_m, st_l, ps, psl, pr, prl, fo, fl,
                   raw_sem, new_sem, q_send, q_recv, kv_send, k_recv, v_recv, p_send, p_recv, f_send, f_recv):
     tok, kvh, ratio, dim = q_hbm.shape
@@ -125,9 +125,13 @@
         for cp in kv_copies(h):
             cp.start()
 
-    def item(s):
-        second = lax.div(s, 4 * half)
-        slot = lax.rem(s + second * 2 * half, 4 * half)
+    n_pairs = 4 * half
+
+    def pair(i):
+        second = lax.div(i, 2 * half)
+        j = i - second * 2 * half
+        late = lax.rem(2 * j + half, 2 * half) + jnp.where(j < half, 2 * half, 0)
+        slot = jnp.where(second == 1, late, 2 * j)
         h = lax.rem(slot, half)
         kv = jnp.where(second == 1, kvh + h, half * core + h)
         owner = jnp.where(second == 1, mate, me)
@@ -155,62 +159,67 @@
         return t if mx is None else jnp.maximum(mx, t)
 
     def first_scores():
-        f, slot, kv, owner, home = item(0)
-        qv = qt[slot]
-        mx = None
-        for c in range(chunks):
-            st = qk_tile(kv, f, c, qv)
-            s0[pl.ds(c * TK, TK), :] = st
-            mx = fold_max(mx, st)
-        st = qk_new(kv, owner, home, qv)
-        s0[pl.ds(cache, tok), :] = st
-        m0[...] = fold_max(mx, st)
-
-    def step(s, sc, sn, mc, mn):
-        nxt = lax.rem(s + 1, 8 * half)
-        f_n, slot_n, kv_n, owner_n, home_n = item(nxt)
-        _, slot, kv, _, _ = item(s)
-
-        ahead = s + 2
+        f, slot, kv, owner, home = pair(0)
+        for e in range(2):
+            qv = qt[slot + e]
+            mx = None
+            for c in range(chunks):
+                st = qk_tile(kv + e, f, c, qv)
+                s_even[e][pl.ds(c * TK, TK), :] = st
+                mx = fold_max(mx, st)
+            st = qk_new(kv + e, owner, home, qv)
+            s_even[e][pl.ds(cache, tok), :] = st
+            m_even[e][...] = fold_max(mx, st)
+
+    def region(i, sc, sn, mc, mn):
+        nxt = lax.rem(i + 1, n_pairs)
+        f_n, slot_n, kv_n, owner_n, home_n = pair(nxt)
+        _, slot, kv, _, _ = pair(i)
+        ahead = 2 * i + 4
 
         @pl.when(jnp.logical_and(ahead >= half, ahead < 4 * half))
         def _():
-            pltpu.make_async_copy(qraw.at[ahead], qraw.at[ahead], q_recv.at[ahead]).wait()
-
-        @pl.when(jnp.logical_and(nxt >= 4 * half, nxt < 5 * half))
+            for e in range(2):
+                pltpu.make_async_copy(qraw.at[ahead + e], qraw.at[ahead + e], q_recv.at[ahead + e]).wait()
+
+        @pl.when(jnp.logical_and(nxt >= 2 * half, nxt < 2 * half + half // 2))
         def _():
-            h = nxt - 4 * half
-            pltpu.make_async_copy(kbuf.at[kvh + h], kbuf.at[kvh + h], k_recv.at[h]).wait()
-            pltpu.make_async_copy(vbuf.at[kvh + h], vbuf.at[kvh + h], v_recv.at[h]).wait()
-
-        qv = qt[slot_n]
-        m_old = st_m[slot]
-        m = jnp.maximum(m_old, jnp.max(mc[...], axis=0, keepdims=True) * scale2)
-        decay = jnp.exp2(m_old - m)
-        mx = None
-        l8 = jnp.zeros((8, rows), F32)
-        o = None
+            for e in range(2):
+                h = 2 * (nxt - 2 * half) + e
+                pltpu.make_async_copy(kbuf.at[kvh + h], kbuf.at[kvh + h], k_recv.at[h]).wait()
+                pltpu.make_async_copy(vbuf.at[kvh + h], vbuf.at[kvh + h], v_recv.at[h]).wait()
+
+        qv, m, decay, mx, l8, o = [], [], [], [None] * 2, [], [None] * 2
+        for e in range(2):
+            qv.append(qt[slot_n + e])
+            m_old = st_m[slot + e]
+            m.append(jnp.maximum(m_old, jnp.max(mc[e][...], axis=0, keepdims=True) * scale2))
+            decay.append(jnp.exp2(m_old - m[e]))
+            l8.append(jnp.zeros((8, rows), F32))
         for c in range(chunks):
             sl = pl.ds(c * TK, TK)
-            st = qk_tile(kv_n, f_n, c, qv)
-            p = jnp.exp2(sc[sl, :] * scale2 - m)
-            sn[sl, :] = st
-            mx = fold_max(mx, st)
-            l8 = l8 + jnp.sum(p.reshape(TK // 8, 8, rows), axis=0)
-            t = jnp.dot(vbuf[kv, :, sl], p.astype(BF), preferred_element_type=F32)
-            o = t if o is None else o + t
-        st = qk_new(kv_n, owner_n, home_n, qv)
+            for e in range(2):
+                st = qk_tile(kv_n + e, f_n, c, qv[e])
+                p = jnp.exp2(sc[e][sl, :] * scale2 - m[e])
+                sn[e][sl, :] = st
+                mx[e] = fold_max(mx[e], st)
+                l8[e] = l8[e] + jnp.sum(p.reshape(TK // 8, 8, rows), axis=0)
+                t = jnp.dot(vbuf[kv + e, :, sl], p.astype(BF), preferred_element_type=F32)
+                o[e] = t if o[e] is None else o[e] + t
         sl = pl.ds(cache, tok)
-        p = jnp.exp2(sc[sl, :] * scale2 - m)
-        sn[sl, :] = st
-        mn[...] = fold_max(mx, st)
-        l8 = l8 + jnp.sum(p.reshape(tok // 8, 8, rows), axis=0)
-        pb = jnp.concatenate([p.astype(BF), jnp.zeros((dim - tok, rows), BF)], axis=0)
-        o = o + jnp.dot(vbuf[kv, :, pl.ds(cache, dim)], pb, preferred_element_type=F32)
-        st_o[slot] = st_o[slot] * decay + o
-        st_l[slot] = st_l[slot] * decay + jnp.sum(l8, axis=0, keepdims=True)
-        st_m[slot] = m
-        load_q(jnp.minimum(ahead, 4 * half - 1))
+        for e in range(2):
+            st = qk_new(kv_n + e, owner_n, home_n, qv[e])
+            p = jnp.exp2(sc[e][sl, :] * scale2 - m[e])
+            sn[e][sl, :] = st
+            mn[e][...] = fold_max(mx[e], st)
+            l8[e] = l8[e] + jnp.sum(p.reshape(tok // 8, 8, rows), axis=0)
+            pb = jnp.concatenate([p.astype(BF), jnp.zeros((dim - tok, rows), BF)], axis=0)
+            o[e] = o[e] + jnp.dot(vbuf[kv + e, :, pl.ds(cache, dim)], pb, preferred_element_type=F32)
+        for e in range(2):
+            st_o[slot + e] = st_o[slot + e] * decay[e] + o[e]
+            st_l[slot + e] = st_l[slot + e] * decay[e] + jnp.sum(l8[e], axis=0, keepdims=True)
+            st_m[slot + e] = m[e]
+            load_q(jnp.minimum(ahead, 4 * half - 2) + e)
 
     def partial_copies(u):
         return (pltpu.make_async_remote_copy(
@@ -234,52 +243,59 @@
                     src_ref=fl.at[u], dst_ref=lse_hbm.at[hh], send_sem=f_send.at[1, u],
                     recv_sem=f_recv.at[1, u - half], device_id={'cp': mate}, device_id_type=MESH))
 
-    def finish(s):
-        @pl.when(jnp.logical_and(s >= 4 * half, s < 6 * half))
+    def finish(i):
+        _, slot, _, _, _ = pair(i)
+
+        @pl.when(jnp.logical_and(i >= 2 * half, i < 3 * half))
         def _():
-            u = s - 4 * half
-            slot = u + 2 * half
-            l = st_l[slot]
-            ps[u] = (st_o[slot] * (1.0 / l)).astype(BF)
-            psl[u] = st_m[slot] + jnp.log2(l)
-            for cp in partial_copies(u):
-                cp.start()
-
-        @pl.when(s >= 6 * half)
+            u = slot - 2 * half
+            for e in range(2):
+                l = st_l[slot + e]
+                ps[u + e] = (st_o[slot + e] * (1.0 / l)).astype(BF)
+                psl[u + e] = st_m[slot + e] + jnp.log2(l)
+            for e in range(2):
+                for cp in partial_copies(u + e):
+                    cp.start()
+
+        @pl.when(i >= 3 * half)
         def _():
-            u = s - 6 * half
-            for cp in partial_copies(u):
-                cp.wait_recv()
-            m_a, m_b = st_m[u], prl[u]
-            m = jnp.maximum(m_a, m_b)
-            a, b = jnp.exp2(m_a - m), jnp.exp2(m_b - m)
-            l = st_l[u] * a + b
-            inv = 1.0 / l
-            o = st_o[u] * (a * inv) + pr[u].astype(F32) * (b * inv)
-            fo[u] = o.T.astype(BF).reshape(tok, ratio, dim)
-            fl[u] = (m + jnp.log2(l)) * math.log(2.0)
+            u = slot
+            for e in range(2):
+                for cp in partial_copies(u + e):
+                    cp.wait_recv()
+            for e in range(2):
+                m_a, m_b = st_m[u + e], prl[u + e]
+                m = jnp.maximum(m_a, m_b)
+                a, b = jnp.exp2(m_a - m), jnp.exp2(m_b - m)
+                l = st_l[u + e] * a + b
+                inv = 1.0 / l
+                o = st_o[u + e] * (a * inv) + pr[u + e].astype(F32) * (b * inv)
+                fo[u + e] = o.T.astype(BF).reshape(tok, ratio, dim)
+                fl[u + e] = (m + jnp.log2(l)) * math.log(2.0)
 
             @pl.when(u < half)
             def _():
-                for cp in own_out(u):
-                    cp.start()
+                for e in range(2):
+                    for cp in own_out(u + e):
+                        cp.start()
 
             @pl.when(u >= half)
             def _():
-                for cp in mate_out(u):
-                    cp.start()
+                for e in range(2):
+                    for cp in mate_out(u + e):
+                        cp.start()
 
     for h in range(half):
         own_q(h).wait()
-    load_q(0)
-    load_q(1)
+    for h in range(half):
+        load_q(h)
     first_scores()
 
-    @pl.loop(0, 4 * half)
+    @pl.loop(0, n_pairs // 2)
     def _(i):
-        step(2 * i, s0, s1, m0, m1)
+        region(2 * i, s_even, s_odd, m_even, m_odd)
         finish(2 * i)
-        step(2 * i + 1, s1, s0, m1, m0)
+        region(2 * i + 1, s_odd, s_even, m_odd, m_even)
         finish(2 * i + 1)
 
     for k in range(3):
@@ -297,6 +313,31 @@
         for cp in mate_out(u + half):
             cp.wait_send()
             cp.wait_recv()
+
+
+def place_kernel(out_ref, lse_ref, out_hbm, lse_out, buf, sem):
+    kvh, _, rows = lse_ref.shape
+    tok, heads = lse_out.shape
+    ratio = heads // kvh
+    parts = sem.shape[1]
+    step = tok // parts
+    reads = [pltpu.make_async_copy(out_ref.at[pl.ds(j * step, step)], buf.at[pl.ds(j * step, step)], sem.at[0, j]) for j in range(parts)]
+    writes = [pltpu.make_async_copy(buf.at[pl.ds(j * step, step)], out_hbm.at[pl.ds(j * step, step)], sem.at[1, j]) for j in range(parts)]
+    for cp in reads:
+        cp.start()
+    x = lse_ref[...].reshape(kvh, rows)
+    lane = lax.broadcasted_iota(jnp.int32, (kvh, heads), 1) // ratio
+    head = lax.broadcasted_iota(jnp.int32, (kvh, heads), 0)
+    per = heads // ratio
+    blocks = [pltpu.roll(x[:, b * heads:(b + 1) * heads], 0, 1, stride=ratio, stride_axis=0) for b in range(tok // per)]
+    for t in range(tok):
+        turned = pltpu.roll(blocks[t // per], (heads - (t % per) * ratio) % heads, 1)
+        lse_out[pl.ds(t, 1), :] = jnp.sum(jnp.where(lane == head, turned, 0.0), axis=0, keepdims=True)
+    for r, w in zip(reads, writes):
+        r.wait()
+        w.start()
+    for w in writes:
+        w.wait()
 
 
 def solution(mesh):
@@ -321,10 +362,10 @@
             pltpu.VMEM((2, cache, dim), BF),
             pltpu.VMEM((4 * half, tok, ratio, dim), BF),
             pltpu.VMEM((4 * half, 2 * dim, rows), BF),
-            pltpu.VMEM((cache + tok, rows), F32),
-            pltpu.VMEM((cache + tok, rows), F32),
-            pltpu.VMEM((8, rows), F32),
-            pltpu.VMEM((8, rows), F32),
+            (pltpu.VMEM((cache + tok, rows), F32),) * 2,
+            (pltpu.VMEM((cache + tok, rows), F32),) * 2,
+            (pltpu.VMEM((8, rows), F32),) * 2,
+            (pltpu.VMEM((8, rows), F32),) * 2,
             pltpu.VMEM((4 * half, dim, rows), F32),
             pltpu.VMEM((4 * half, 1, rows), F32),
             pltpu.VMEM((4 * half, 1, rows), F32),
@@ -349,8 +390,16 @@
             name='attend',
         )(queries.reshape(tok, kvh, ratio, dim), key_new.reshape(tok * kvh, dim), value_new.reshape(tok * kvh, dim),
           key_cache.reshape(cache * kvh, dim), value_cache.reshape(cache * kvh, dim), prefix_len)
-        row_lse = lse.reshape(kvh, tok, ratio).transpose(1, 0, 2).reshape(tok, heads)
-        return out.reshape(tok, heads, dim), row_lse
+        vmem = pl.BlockSpec(memory_space=pltpu.VMEM)
+        out, row_lse = pl.pallas_call(
+            place_kernel,
+            out_shape=(jax.ShapeDtypeStruct((tok, heads, dim), BF), jax.ShapeDtypeStruct((tok, heads), F32)),
+            in_specs=[hbm, vmem],
+            out_specs=(hbm, vmem),
+            scratch_shapes=[pltpu.VMEM((tok, heads, dim), BF), dma((2, 4))],
+            name='place',
+        )(out.reshape(tok, heads, dim), lse)
+        return out, row_lse
 
     return jax.shard_map(local, mesh=mesh, in_specs=(tok_spec, tok_spec, tok_spec, tok_spec, tok_spec, P('dp')),
                          out_specs=(tok_spec, tok_spec), check_vma=False)

time: 50.2 us -> 46.5 us (0.926)
  local copies, waits for them, and re-layouts: 2.66 us -> 0 us
  other arithmetic: 0.72 us -> 0 us
    pallas_call x1, Pallas kernels: 45.3 us -> 41.9 us  [local(): pl.pallas_call(attend_kernel, out_shape=(jax.ShapeDtypeStruct((tok, kvh,...]
    pallas_call x0 -> x1, Pallas kernels: none -> 3.14 us  [local(): pl.pallas_call(place_kernel, out_shape=(jax.ShapeDtypeStruct((tok, heads,...]
    unnamed x1 -> x0, local copies, waits for them, and re-layouts: 1.88 us -> none
    reshape x2 -> x0, local copies, waits for them, and re-layouts: 0.76 us -> none  [local(): lse.reshape(kvh, tok, ratio).transpose(1, 0, 2).reshape(tok, heads)]
    pallas_call x1 -> x0, other arithmetic: 0.72 us -> none  [local(): pl.pallas_call(attend_kernel, out_shape=(jax.ShapeDtypeStruct((tok, kvh,...]
where the time goes in v2:
time: 46.5 us; the launch traced here: 46.3 us
  Pallas kernels  45 us (97%)
  between operations  1.29 us (3%)
    pallas_call x1, Pallas kernels, local(): pl.pallas_call(attend_kernel, out_shape=(jax.ShapeDtypeStruct((tok, kvh,...  41.9 us
    pallas_call x1, Pallas kernels, local(): pl.pallas_call(place_kernel, out_shape=(jax.ShapeDtypeStruct((tok, heads,...  3.14 us

profile of v2, /device:TPU:0, one launch (start us, length us, event | category | flops | bytes accessed | tf_op | source)
XLA Modules:
  0.0 46.3 jit_solution(11681715433958424857)
XLA Ops:
  1.3 41.9 %attend.1 = (bf16[16,8,16,128]{3,2,1,0:T(8,128)(2,1)}, f32[8,1,256]{2,1,0:T(1,128)}) custom-call(bf16[16,8,16,128]{3,2,1,0:T(8,128)(2,1)} %bitcast.9, bf16[128,128]{1,0:T(8,128)(2,1)} %bitcast.10, bf16[128,128]{1,0:T(8,128)(2,1)} %bitcast.11, bf16[24576,128]{1,0:T(8,128)(2,1)} %bitcast.7, bf16[24576,128]{1,0:T(8,128)(2,1)} %bitcast.8, s32[1]{0:T(128)S(6)} %copy.8.plen_ref), custom_call_target="tpu_custom_call" | custom-call | flops 12884901888 | bytes 12582912 | tf_op jit(solution)/shard_map/attend/pallas_call | solution.py:382
  43.2 3.1 %place.1 = (bf16[16,128,128]{2,1,0:T(8,128)(2,1)}, f32[16,128]{1,0:T(8,128)}) custom-call(bf16[16,128,128]{2,1,0:T(8,128)(2,1)} %bitcast.6, f32[8,1,256]{2,1,0:T(1,128)} %get-tuple-element.5.lse_ref), custom_call_target="tpu_custom_call" | custom-call | tf_op jit(solution)/shard_map/place/pallas_call | solution.py:394

commit v3 on v2

--- a/solution.py
+++ b/solution.py
@@ -16,7 +16,7 @@
 F32 = jnp.float32
 
 
-def attend_kernel(q_hbm, kn_hbm, vn_hbm, kc_hbm, vc_hbm, plen_ref, out_hbm, lse_hbm,
+def attend_kernel(q_hbm, kn_hbm, vn_hbm, kc_hbm, vc_hbm, plen_ref, out_ref, lse_ref,
                   raw_k, raw_v, new_k, new_v, kbuf, vbuf, bias, qraw, qt, s_even, s_odd, m_even, m_odd,
                   st_o, st_m, st_l, ps, psl, pr, prl, fo, fl,
                   raw_sem, new_sem, q_send, q_recv, kv_send, k_recv, v_recv, p_send, p_recv, f_send, f_recv):
@@ -128,10 +128,14 @@
     n_pairs = 4 * half
 
     def pair(i):
-        second = lax.div(i, 2 * half)
-        j = i - second * 2 * half
-        late = lax.rem(2 * j + half, 2 * half) + jnp.where(j < half, 2 * half, 0)
-        slot = jnp.where(second == 1, late, 2 * j)
+        q = half // 2
+        late = lax.rem(2 * (i - 3 * q - 1) + half, 2 * half) + 2 * half
+        last = lax.rem(2 * (i - 6 * q) + half, 2 * half)
+        slot = jnp.where(i < q + 1, 2 * i,
+               jnp.where(i < 3 * q + 1, 2 * half + 2 * (i - q - 1),
+               jnp.where(i < 5 * q + 1, late,
+               jnp.where(i < 6 * q, 2 * i - 8 * q, last))))
+        second = jnp.where(jnp.logical_or(jnp.logical_and(i >= 3 * q + 1, i < 5 * q + 1), i >= 6 * q), 1, 0)
         h = lax.rem(slot, half)
         kv = jnp.where(second == 1, kvh + h, half * core + h)
         owner = jnp.where(second == 1, mate, me)
@@ -175,17 +179,19 @@
         nxt = lax.rem(i + 1, n_pairs)
         f_n, slot_n, kv_n, owner_n, home_n = pair(nxt)
         _, slot, kv, _, _ = pair(i)
-        ahead = 2 * i + 4
-
-        @pl.when(jnp.logical_and(ahead >= half, ahead < 4 * half))
+        q = half // 2
+        later = jnp.minimum(i + 2, n_pairs - 1)
+        ahead = pair(later)[1]
+
+        @pl.when(jnp.logical_or(i + 2 == 6 * q - 1, jnp.logical_and(i + 2 >= q, i + 2 < 3 * q + 1)))
         def _():
             for e in range(2):
                 pltpu.make_async_copy(qraw.at[ahead + e], qraw.at[ahead + e], q_recv.at[ahead + e]).wait()
 
-        @pl.when(jnp.logical_and(nxt >= 2 * half, nxt < 2 * half + half // 2))
+        @pl.when(jnp.logical_and(nxt >= 3 * q + 1, nxt < 4 * q + 1))
         def _():
             for e in range(2):
-                h = 2 * (nxt - 2 * half) + e
+                h = 2 * (nxt - 3 * q - 1) + e
                 pltpu.make_async_copy(kbuf.at[kvh + h], kbuf.at[kvh + h], k_recv.at[h]).wait()
                 pltpu.make_async_copy(vbuf.at[kvh + h], vbuf.at[kvh + h], v_recv.at[h]).wait()
 
@@ -219,7 +225,7 @@
             st_o[slot + e] = st_o[slot + e] * decay[e] + o[e]
             st_l[slot + e] = st_l[slot + e] * decay[e] + jnp.sum(l8[e], axis=0, keepdims=True)
             st_m[slot + e] = m[e]
-            load_q(jnp.minimum(ahead, 4 * half - 2) + e)
+            load_q(ahead + e)
 
     def partial_copies(u):
         return (pltpu.make_async_remote_copy(
@@ -229,24 +235,21 @@
                     src_ref=psl.at[u], dst_ref=prl.at[u], send_sem=p_send.at[1, u], recv_sem=p_recv.at[1, u],
                     device_id={'cp': far}, device_id_type=MESH))
 
-    def own_out(u):
-        hh = half * core + u
-        return (pltpu.make_async_copy(fo.at[u], out_hbm.at[:, hh], f_send.at[0, u]),
-                pltpu.make_async_copy(fl.at[u], lse_hbm.at[hh], f_send.at[1, u]))
-
     def mate_out(u):
         hh = half * core + u - half
         return (pltpu.make_async_remote_copy(
-                    src_ref=fo.at[u], dst_ref=out_hbm.at[:, hh], send_sem=f_send.at[0, u],
+                    src_ref=fo.at[u - half], dst_ref=out_ref.at[:, hh], send_sem=f_send.at[0, u - half],
                     recv_sem=f_recv.at[0, u - half], device_id={'cp': mate}, device_id_type=MESH),
                 pltpu.make_async_remote_copy(
-                    src_ref=fl.at[u], dst_ref=lse_hbm.at[hh], send_sem=f_send.at[1, u],
+                    src_ref=fl.at[u - half], dst_ref=lse_ref.at[hh], send_sem=f_send.at[1, u - half],
                     recv_sem=f_recv.at[1, u - half], device_id={'cp': mate}, device_id_type=MESH))
 
     def finish(i):
         _, slot, _, _, _ = pair(i)
 
-        @pl.when(jnp.logical_and(i >= 2 * half, i < 3 * half))
+        q = half // 2
+
+        @pl.when(jnp.logical_and(i >= 3 * q + 1, i < 5 * q + 1))
         def _():
             u = slot - 2 * half
             for e in range(2):
@@ -257,12 +260,13 @@
                 for cp in partial_copies(u + e):
                     cp.start()
 
-        @pl.when(i >= 3 * half)
+        @pl.when(i >= 6 * q)
         def _():
             u = slot
             for e in range(2):
                 for cp in partial_copies(u + e):
                     cp.wait_recv()
+            done = []
             for e in range(2):
                 m_a, m_b = st_m[u + e], prl[u + e]
                 m = jnp.maximum(m_a, m_b)
@@ -270,17 +274,19 @@
                 l = st_l[u + e] * a + b
                 inv = 1.0 / l
                 o = st_o[u + e] * (a * inv) + pr[u + e].astype(F32) * (b * inv)
-                fo[u + e] = o.T.astype(BF).reshape(tok, ratio, dim)
-                fl[u + e] = (m + jnp.log2(l)) * math.log(2.0)
+                done.append((o.T.astype(BF).reshape(tok, ratio, dim), (m + jnp.log2(l)) * math.log(2.0)))
 
             @pl.when(u < half)
             def _():
                 for e in range(2):
-                    for cp in own_out(u + e):
-                        cp.start()
+                    out_ref[:, half * core + u + e] = done[e][0]
+                    lse_ref[half * core + u + e] = done[e][1]
 
             @pl.when(u >= half)
             def _():
+                for e in range(2):
+                    fo[u - half + e] = done[e][0]
+                    fl[u - half + e] = done[e][1]
                 for e in range(2):
                     for cp in mate_out(u + e):
                         cp.start()
@@ -308,23 +314,17 @@
         for cp in partial_copies(u):
             cp.wait_send()
     for u in range(half):
-        for cp in own_out(u):
-            cp.wait()
         for cp in mate_out(u + half):
             cp.wait_send()
             cp.wait_recv()
 
 
-def place_kernel(out_ref, lse_ref, out_hbm, lse_out, buf, sem):
+def place_kernel(out_ref, lse_ref, out_hbm, lse_hbm, lse_buf, sem):
     kvh, _, rows = lse_ref.shape
-    tok, heads = lse_out.shape
+    tok, heads = lse_buf.shape
     ratio = heads // kvh
-    parts = sem.shape[1]
-    step = tok // parts
-    reads = [pltpu.make_async_copy(out_ref.at[pl.ds(j * step, step)], buf.at[pl.ds(j * step, step)], sem.at[0, j]) for j in range(parts)]
-    writes = [pltpu.make_async_copy(buf.at[pl.ds(j * step, step)], out_hbm.at[pl.ds(j * step, step)], sem.at[1, j]) for j in range(parts)]
-    for cp in reads:
-        cp.start()
+    write = pltpu.make_async_copy(out_ref, out_hbm, sem.at[0])
+    write.start()
     x = lse_ref[...].reshape(kvh, rows)
     lane = lax.broadcasted_iota(jnp.int32, (kvh, heads), 1) // ratio
     head = lax.broadcasted_iota(jnp.int32, (kvh, heads), 0)
@@ -332,12 +332,11 @@
     blocks = [pltpu.roll(x[:, b * heads:(b + 1) * heads], 0, 1, stride=ratio, stride_axis=0) for b in range(tok // per)]
     for t in range(tok):
         turned = pltpu.roll(blocks[t // per], (heads - (t % per) * ratio) % heads, 1)
-        lse_out[pl.ds(t, 1), :] = jnp.sum(jnp.where(lane == head, turned, 0.0), axis=0, keepdims=True)
-    for r, w in zip(reads, writes):
-        r.wait()
-        w.start()
-    for w in writes:
-        w.wait()
+        lse_buf[pl.ds(t, 1), :] = jnp.sum(jnp.where(lane == head, turned, 0.0), axis=0, keepdims=True)
+    lse_write = pltpu.make_async_copy(lse_buf, lse_hbm, sem.at[1])
+    lse_write.start()
+    write.wait()
+    lse_write.wait()
 
 
 def solution(mesh):
@@ -351,7 +350,8 @@
         rows = tok * ratio
         n_raw = 6
         dma = pltpu.SemaphoreType.DMA
-        hbm = pl.BlockSpec(memory_space=pl.ANY)
+        hbm = pl.BlockSpec(memory_space=pltpu.HBM)
+        vmem = pl.BlockSpec(memory_space=pltpu.VMEM)
         scratch = [
             pltpu.VMEM((cache * kvh, dim), BF),
             pltpu.VMEM((cache * kvh, dim), BF),
@@ -373,30 +373,30 @@
             pltpu.VMEM((2 * half, 1, rows), F32),
             pltpu.VMEM((2 * half, dim, rows), BF),
             pltpu.VMEM((2 * half, 1, rows), F32),
-            pltpu.VMEM((2 * half, tok, ratio, dim), BF),
-            pltpu.VMEM((2 * half, 1, rows), F32),
+            pltpu.VMEM((half, tok, ratio, dim), BF),
+            pltpu.VMEM((half, 1, rows), F32),
             dma((2, n_raw)), dma((2,)), dma((3 * half,)), dma((4 * half,)), dma((2, half)), dma((half,)), dma((half,)),
-            dma((2, 2 * half)), dma((2, 2 * half)), dma((2, 2 * half)), dma((2, half)),
+            dma((2, 2 * half)), dma((2, 2 * half)), dma((2, half)), dma((2, half)),
         ]
         flops = 4 * heads * tok * 4 * cache * dim
         out, lse = pl.pallas_call(
             attend_kernel,
-            out_shape=(jax.ShapeDtypeStruct((tok, kvh, ratio, dim), BF), jax.ShapeDtypeStruct((kvh, 1, rows), F32)),
+            out_shape=(pltpu.VMEM((tok, kvh, ratio, dim), BF), pltpu.VMEM((kvh, 1, rows), F32)),
             in_specs=[hbm] * 5 + [pl.BlockSpec(memory_space=pltpu.SMEM)],
-            out_specs=(hbm, hbm),
+            out_specs=(vmem, vmem),
             scratch_shapes=scratch,
-            compiler_params=pltpu.CompilerParams(collective_id=0, has_side_effects=True, vmem_limit_bytes=63 * 2 ** 20),
+            compiler_params=pltpu.CompilerParams(collective_id=0, has_side_effects=True, vmem_limit_bytes=60 * 2 ** 20),
             cost_estimate=pl.CostEstimate(flops=flops, bytes_accessed=4 * cache * kvh * dim, transcendentals=heads * tok * 4 * cache),
             name='attend',
         )(queries.reshape(tok, kvh, ratio, dim), key_new.reshape(tok * kvh, dim), value_new.reshape(tok * kvh, dim),
           key_cache.reshape(cache * kvh, dim), value_cache.reshape(cache * kvh, dim), prefix_len)
-        vmem = pl.BlockSpec(memory_space=pltpu.VMEM)
         out, row_lse = pl.pallas_call(
             place_kernel,
             out_shape=(jax.ShapeDtypeStruct((tok, heads, dim), BF), jax.ShapeDtypeStruct((tok, heads), F32)),
-            in_specs=[hbm, vmem],
-            out_specs=(hbm, vmem),
-            scratch_shapes=[pltpu.VMEM((tok, heads, dim), BF), dma((2, 4))],
+            in_specs=[vmem, vmem],
+            out_specs=(hbm, hbm),
+            scratch_shapes=[pltpu.VMEM((tok, heads), F32), dma((2,))],
+            compiler_params=pltpu.CompilerParams(vmem_limit_bytes=2 * 2 ** 20),
             name='place',
         )(out.reshape(tok, heads, dim), lse)
         return out, row_lse

time: 46.5 us -> 41.9 us (0.901)
  Pallas kernels: 45 us -> 40.5 us
    pallas_call x1, Pallas kernels: 3.14 us -> 0.82 us  [local(): pl.pallas_call(place_kernel, out_shape=(jax.ShapeDtypeStruct((tok, heads,...]
    pallas_call x1, Pallas kernels: 41.9 us -> 39.7 us  [local(): pl.pallas_call(attend_kernel, out_shape=(pltpu.VMEM((tok, kvh, ratio, dim...]
where the time goes in v3:
time: 41.9 us; the launch traced here: 41.8 us
  Pallas kernels  40.5 us (97%)
  between operations  1.29 us (3%)
    pallas_call x1, Pallas kernels, local(): pl.pallas_call(attend_kernel, out_shape=(pltpu.VMEM((tok, kvh, ratio, dim...  39.7 us

profile of v3, /device:TPU:0, one launch (start us, length us, event | category | flops | bytes accessed | tf_op | source)
XLA Modules:
  0.0 41.8 jit_solution(11206617760920462882)
XLA Ops:
  1.3 39.7 %attend.1 = (bf16[16,8,16,128]{3,2,1,0:T(8,128)(2,1)S(1)}, f32[8,1,256]{2,1,0:T(1,128)S(1)}) custom-call(bf16[16,8,16,128]{3,2,1,0:T(8,128)(2,1)} %bitcast.9, bf16[128,128]{1,0:T(8,128)(2,1)} %bitcast.10, bf16[128,128]{1,0:T(8,128)(2,1)} %bitcast.11, bf16[24576,128]{1,0:T(8,128)(2,1)} %bitcast.7, bf16[24576,128]{1,0:T(8,128)(2,1)} %bitcast.8, s32[1]{0:T(128)S(6)} %copy.8.plen_ref), custom_call_target="tpu_custom_call" | custom-call | flops 12884901888 | bytes 12582912 | tf_op jit(solution)/shard_map/attend/pallas_call | solution.py:382
  41.0 0.8 %place.1 = (bf16[16,128,128]{2,1,0:T(8,128)(2,1)}, f32[16,128]{1,0:T(8,128)}) custom-call(bf16[16,128,128]{2,1,0:T(8,128)(2,1)S(1)} %bitcast.6, f32[8,1,256]{2,1,0:T(1,128)S(1)} %get-tuple-element.5.lse_ref), custom_call_target="tpu_custom_call" | custom-call | tf_op jit(solution)/shard_map/place/pallas_call | solution.py:393

commit v4 on v3

--- a/solution.py
+++ b/solution.py
@@ -13,11 +13,32 @@
 TK = 256
 PREP = 128
 BF = jnp.bfloat16
+SEQ = ((0, 0), (2, 0), (4, 0), (12, 0), (14, 0), (12, 1), (8, 0), (14, 1),
+       (10, 0), (8, 1), (10, 1), (6, 0), (4, 1), (6, 1), (0, 1), (2, 1))
 F32 = jnp.float32
 
 
+def _packed(part):
+    v = sum((slot // 2 + 8 * second) << (4 * k) for k, (slot, second) in enumerate(part))
+    return v - (1 << 32) if v >= 1 << 31 else v
+
+
+ORDER = (_packed(SEQ[:8]), _packed(SEQ[8:]))
+Q_PAIRS = tuple(SEQ.index((s, 0)) for s in range(4, 16, 2))
+KV_PAIRS = tuple(next(k for k, (s, f) in enumerate(SEQ) if f and s % 4 == h) for h in (0, 2))
+R_PAIRS = tuple(k for k, (s, f) in enumerate(SEQ) if f and s >= 8)
+L_PAIRS = tuple(k for k, (s, f) in enumerate(SEQ) if f and s < 8)
+
+
+def among(i, ks):
+    hit = i == ks[0]
+    for k in ks[1:]:
+        hit = jnp.logical_or(hit, i == k)
+    return hit
+
+
 def attend_kernel(q_hbm, kn_hbm, vn_hbm, kc_hbm, vc_hbm, plen_ref, out_ref, lse_ref,
-                  raw_k, raw_v, new_k, new_v, kbuf, vbuf, bias, qraw, qt, s_even, s_odd, m_even, m_odd,
+                  raw_k, raw_v, new_k, new_v, kbuf, vbuf, bias, qraw, qt, sbuf, mbuf,
                   st_o, st_m, st_l, ps, psl, pr, prl, fo, fl,
                   raw_sem, new_sem, q_send, q_recv, kv_send, k_recv, v_recv, p_send, p_recv, f_send, f_recv):
     tok, kvh, ratio, dim = q_hbm.shape
@@ -71,8 +92,8 @@
     pl.semaphore_wait(barrier, 3)
 
     def q_copy(k, h):
-        peer, base = ((far, 2 * half), (far_other, 3 * half), (mate, half))[k]
-        peer_core = (core, 1 - core, 1 - core)[k]
+        peer, base = ((far_other, 3 * half), (far, 2 * half), (mate, half))[k]
+        peer_core = (1 - core, core, 1 - core)[k]
         return pltpu.make_async_remote_copy(
             src_ref=q_hbm.at[:, half * peer_core + h], dst_ref=qraw.at[base + h],
             send_sem=q_send.at[k * half + h], recv_sem=q_recv.at[base + h],
@@ -99,6 +120,22 @@
         kbuf[h, pl.ds(cache, tok), :] = kt[h]
         vpad = jnp.concatenate([vt[h].astype(F32), jnp.zeros((dim - tok, dim), F32)], axis=0)
         vbuf[h, :, pl.ds(cache, dim)] = vpad.T.astype(BF)
+    def kv_parts(h, lo, n):
+        src = half * (1 - core) + h
+        to = dict(device_id={'cp': mate}, device_id_type=MESH)
+        k_rows, v_lanes = pl.ds(lo, min(n, cache + tok - lo)), pl.ds(lo, n)
+        return (pltpu.make_async_remote_copy(
+                    src_ref=kbuf.at[src, k_rows], dst_ref=kbuf.at[kvh + h, k_rows],
+                    send_sem=kv_send.at[0, h], recv_sem=k_recv.at[h], **to),
+                pltpu.make_async_remote_copy(
+                    src_ref=vbuf.at[src, :, v_lanes], dst_ref=vbuf.at[kvh + h, :, v_lanes],
+                    send_sem=kv_send.at[1, h], recv_sem=v_recv.at[h], **to))
+
+    def kv_start(lo, n):
+        for h in range(half):
+            for cp in kv_parts(h, lo, n):
+                cp.start()
+
     for j in range(n_raw):
         for cp in raw_copy(j):
             cp.wait()
@@ -113,29 +150,17 @@
                 kbuf[h, pl.ds(base, PREP), :] = xk[h]
                 vbuf[h, :, pl.ds(base, PREP)] = xv[h].T
 
-    def kv_copies(h):
-        src = half * (1 - core) + h
-        return tuple(
-            pltpu.make_async_remote_copy(
-                src_ref=buf.at[src], dst_ref=buf.at[kvh + h], send_sem=kv_send.at[w, h], recv_sem=recv.at[h],
-                device_id={'cp': mate}, device_id_type=MESH)
-            for w, (buf, recv) in enumerate(((kbuf, k_recv), (vbuf, v_recv))))
-
-    for h in range(half):
-        for cp in kv_copies(h):
-            cp.start()
+        if j == 0:
+            kv_start(cache, dim)
+        else:
+            kv_start((j - 1) * raw_pos, raw_pos)
 
     n_pairs = 4 * half
 
     def pair(i):
-        q = half // 2
-        late = lax.rem(2 * (i - 3 * q - 1) + half, 2 * half) + 2 * half
-        last = lax.rem(2 * (i - 6 * q) + half, 2 * half)
-        slot = jnp.where(i < q + 1, 2 * i,
-               jnp.where(i < 3 * q + 1, 2 * half + 2 * (i - q - 1),
-               jnp.where(i < 5 * q + 1, late,
-               jnp.where(i < 6 * q, 2 * i - 8 * q, last))))
-        second = jnp.where(jnp.logical_or(jnp.logical_and(i >= 3 * q + 1, i < 5 * q + 1), i >= 6 * q), 1, 0)
+        code = lax.shift_right_logical(jnp.where(i < 8, ORDER[0], ORDER[1]), 4 * lax.rem(i, 8))
+        slot = 2 * jnp.bitwise_and(code, 7)
+        second = lax.div(jnp.bitwise_and(code, 15), 8)
         h = lax.rem(slot, half)
         kv = jnp.where(second == 1, kvh + h, half * core + h)
         owner = jnp.where(second == 1, mate, me)
@@ -169,63 +194,70 @@
             mx = None
             for c in range(chunks):
                 st = qk_tile(kv + e, f, c, qv)
-                s_even[e][pl.ds(c * TK, TK), :] = st
+                sbuf[e][pl.ds(c * TK, TK), :] = st
                 mx = fold_max(mx, st)
             st = qk_new(kv + e, owner, home, qv)
-            s_even[e][pl.ds(cache, tok), :] = st
-            m_even[e][...] = fold_max(mx, st)
-
-    def region(i, sc, sn, mc, mn):
-        nxt = lax.rem(i + 1, n_pairs)
-        f_n, slot_n, kv_n, owner_n, home_n = pair(nxt)
+            sbuf[e][pl.ds(cache, tok), :] = st
+            mbuf[e][...] = fold_max(mx, st)
+
+    def wait_inputs(i):
         _, slot, kv, _, _ = pair(i)
-        q = half // 2
-        later = jnp.minimum(i + 2, n_pairs - 1)
-        ahead = pair(later)[1]
-
-        @pl.when(jnp.logical_or(i + 2 == 6 * q - 1, jnp.logical_and(i + 2 >= q, i + 2 < 3 * q + 1)))
+
+        @pl.when(among(i, Q_PAIRS))
         def _():
             for e in range(2):
-                pltpu.make_async_copy(qraw.at[ahead + e], qraw.at[ahead + e], q_recv.at[ahead + e]).wait()
-
-        @pl.when(jnp.logical_and(nxt >= 3 * q + 1, nxt < 4 * q + 1))
+                pltpu.make_async_copy(qraw.at[slot + e], qraw.at[slot + e], q_recv.at[slot + e]).wait()
+
+    def wait_kv(i):
+        _, slot, kv, _, _ = pair(i)
+
+        @pl.when(among(i, KV_PAIRS))
         def _():
             for e in range(2):
-                h = 2 * (nxt - 3 * q - 1) + e
-                pltpu.make_async_copy(kbuf.at[kvh + h], kbuf.at[kvh + h], k_recv.at[h]).wait()
-                pltpu.make_async_copy(vbuf.at[kvh + h], vbuf.at[kvh + h], v_recv.at[h]).wait()
-
-        qv, m, decay, mx, l8, o = [], [], [], [None] * 2, [], [None] * 2
+                pltpu.make_async_copy(kbuf.at[kv + e], kbuf.at[kv + e], k_recv.at[kv + e - kvh]).wait()
+                pltpu.make_async_copy(vbuf.at[kv + e], vbuf.at[kv + e], v_recv.at[kv + e - kvh]).wait()
+
+    def region(r):
+        cur = [2 * r, 2 * r + 1, jnp.minimum(2 * r + 2, n_pairs - 1), jnp.minimum(2 * r + 3, n_pairs - 1)]
+        wait_inputs(2 * r + 2)
+        wait_inputs(2 * r + 3)
+        wait_kv(2 * r + 1)
+        wait_kv(2 * r + 2)
+        info = [pair(c) for c in cur]
+        units = [tuple(x + e if k in (1, 2) else x for k, x in enumerate(info[p])) for p in range(3) for e in range(2)]
         for e in range(2):
-            qv.append(qt[slot_n + e])
-            m_old = st_m[slot + e]
-            m.append(jnp.maximum(m_old, jnp.max(mc[e][...], axis=0, keepdims=True) * scale2))
-            decay.append(jnp.exp2(m_old - m[e]))
-            l8.append(jnp.zeros((8, rows), F32))
-        for c in range(chunks):
-            sl = pl.ds(c * TK, TK)
-            for e in range(2):
-                st = qk_tile(kv_n + e, f_n, c, qv[e])
-                p = jnp.exp2(sc[e][sl, :] * scale2 - m[e])
-                sn[e][sl, :] = st
-                mx[e] = fold_max(mx[e], st)
-                l8[e] = l8[e] + jnp.sum(p.reshape(TK // 8, 8, rows), axis=0)
-                t = jnp.dot(vbuf[kv + e, :, sl], p.astype(BF), preferred_element_type=F32)
-                o[e] = t if o[e] is None else o[e] + t
-        sl = pl.ds(cache, tok)
+            load_q(info[2][1] + e)
+        m_old = [st_m[units[e][1]] for e in range(4)]
+        for e in range(4):
+            _, slot, kv, _, _ = units[e]
+            f_n, slot_n, kv_n, owner_n, home_n = units[e + 2]
+            n = (e + 2) % 4
+            qv = qt[slot_n]
+            m = jnp.maximum(m_old[e], jnp.max(mbuf[e][...], axis=0, keepdims=True) * scale2)
+            decay = jnp.exp2(m_old[e] - m)
+            mx, o, l8 = None, None, jnp.zeros((8, rows), F32)
+            for c in range(chunks):
+                sl = pl.ds(c * TK, TK)
+                st = qk_tile(kv_n, f_n, c, qv)
+                p = jnp.exp2(sbuf[e][sl, :] * scale2 - m)
+                sbuf[n][sl, :] = st
+                mx = fold_max(mx, st)
+                l8 = l8 + jnp.sum(p.reshape(TK // 8, 8, rows), axis=0)
+                t = jnp.dot(vbuf[kv, :, sl], p.astype(BF), preferred_element_type=F32)
+                o = t if o is None else o + t
+            sl = pl.ds(cache, tok)
+            st = qk_new(kv_n, owner_n, home_n, qv)
+            p = jnp.exp2(sbuf[e][sl, :] * scale2 - m)
+            sbuf[n][sl, :] = st
+            mbuf[n][...] = fold_max(mx, st)
+            l8 = l8 + jnp.sum(p.reshape(tok // 8, 8, rows), axis=0)
+            pb = jnp.concatenate([p.astype(BF), jnp.zeros((dim - tok, rows), BF)], axis=0)
+            o = o + jnp.dot(vbuf[kv, :, pl.ds(cache, dim)], pb, preferred_element_type=F32)
+            st_o[slot] = st_o[slot] * decay + o
+            st_l[slot] = st_l[slot] * decay + jnp.sum(l8, axis=0, keepdims=True)
+            st_m[slot] = m
         for e in range(2):
-            st = qk_new(kv_n + e, owner_n, home_n, qv[e])
-            p = jnp.exp2(sc[e][sl, :] * scale2 - m[e])
-            sn[e][sl, :] = st
-            mn[e][...] = fold_max(mx[e], st)
-            l8[e] = l8[e] + jnp.sum(p.reshape(tok // 8, 8, rows), axis=0)
-            pb = jnp.concatenate([p.astype(BF), jnp.zeros((dim - tok, rows), BF)], axis=0)
-            o[e] = o[e] + jnp.dot(vbuf[kv + e, :, pl.ds(cache, dim)], pb, preferred_element_type=F32)
-        for e in range(2):
-            st_o[slot + e] = st_o[slot + e] * decay[e] + o[e]
-            st_l[slot + e] = st_l[slot + e] * decay[e] + jnp.sum(l8[e], axis=0, keepdims=True)
-            st_m[slot + e] = m[e]
-            load_q(ahead + e)
+            load_q(info[3][1] + e)
 
     def partial_copies(u):
         return (pltpu.make_async_remote_copy(
@@ -247,9 +279,7 @@
     def finish(i):
         _, slot, _, _, _ = pair(i)
 
-        q = half // 2
-
-        @pl.when(jnp.logical_and(i >= 3 * q + 1, i < 5 * q + 1))
+        @pl.when(among(i, R_PAIRS))
         def _():
             u = slot - 2 * half
             for e in range(2):
@@ -260,7 +290,7 @@
                 for cp in partial_copies(u + e):
                     cp.start()
 
-        @pl.when(i >= 6 * q)
+        @pl.when(among(i, L_PAIRS))
         def _():
             u = slot
             for e in range(2):
@@ -296,20 +326,20 @@
     for h in range(half):
         load_q(h)
     first_scores()
+    kv_start(cache - raw_pos, raw_pos)
 
     @pl.loop(0, n_pairs // 2)
-    def _(i):
-        region(2 * i, s_even, s_odd, m_even, m_odd)
-        finish(2 * i)
-        region(2 * i + 1, s_odd, s_even, m_odd, m_even)
-        finish(2 * i + 1)
+    def _(r):
+        region(r)
+        finish(2 * r)
+        finish(2 * r + 1)
 
     for k in range(3):
         for h in range(half):
             q_copy(k, h).wait_send()
     for h in range(half):
-        for cp in kv_copies(h):
-            cp.wait_send()
+        pltpu.make_async_copy(kbuf.at[h], kbuf.at[h], kv_send.at[0, h]).wait()
+        pltpu.make_async_copy(vbuf.at[h], vbuf.at[h], kv_send.at[1, h]).wait()
     for u in range(2 * half):
         for cp in partial_copies(u):
             cp.wait_send()
@@ -362,10 +392,8 @@
             pltpu.VMEM((2, cache, dim), BF),
             pltpu.VMEM((4 * half, tok, ratio, dim), BF),
             pltpu.VMEM((4 * half, 2 * dim, rows), BF),
-            (pltpu.VMEM((cache + tok, rows), F32),) * 2,
-            (pltpu.VMEM((cache + tok, rows), F32),) * 2,
-            (pltpu.VMEM((8, rows), F32),) * 2,
-            (pltpu.VMEM((8, rows), F32),) * 2,
+            (pltpu.VMEM((cache + tok, rows), F32),) * 4,
+            (pltpu.VMEM((8, rows), F32),) * 4,
             pltpu.VMEM((4 * half, dim, rows), F32),
             pltpu.VMEM((4 * half, 1, rows), F32),
             pltpu.VMEM((4 * half, 1, rows), F32),

time: 41.9 us -> 46.4 us (1.11)
  Pallas kernels: 40.5 us -> 45 us
    pallas_call x1, Pallas kernels: 39.7 us -> 44.2 us  [local(): pl.pallas_call(attend_kernel, out_shape=(pltpu.VMEM((tok, kvh, ratio, dim...]
where the time goes in v4:
time: 46.4 us; the launch traced here: 46.3 us
  Pallas kernels  45 us (97%)
  between operations  1.29 us (3%)
    pallas_call x1, Pallas kernels, local(): pl.pallas_call(attend_kernel, out_shape=(pltpu.VMEM((tok, kvh, ratio, dim...  44.2 us

profile of v4, /device:TPU:0, one launch (start us, length us, event | category | flops | bytes accessed | tf_op | source)
XLA Modules:
  0.0 46.3 jit_solution(13635286621036122226)
XLA Ops:
  1.3 44.2 %attend.1 = (bf16[16,8,16,128]{3,2,1,0:T(8,128)(2,1)S(1)}, f32[8,1,256]{2,1,0:T(1,128)S(1)}) custom-call(bf16[16,8,16,128]{3,2,1,0:T(8,128)(2,1)} %bitcast.9, bf16[128,128]{1,0:T(8,128)(2,1)} %bitcast.10, bf16[128,128]{1,0:T(8,128)(2,1)} %bitcast.11, bf16[24576,128]{1,0:T(8,128)(2,1)} %bitcast.7, bf16[24576,128]{1,0:T(8,128)(2,1)} %bitcast.8, s32[1]{0:T(128)S(6)} %copy.8.plen_ref), custom_call_target="tpu_custom_call" | custom-call | flops 12884901888 | bytes 12582912 | tf_op jit(solution)/shard_map/attend/pallas_call | solution.py:410
  45.5 0.8 %place.1 = (bf16[16,128,128]{2,1,0:T(8,128)(2,1)}, f32[16,128]{1,0:T(8,128)}) custom-call(bf16[16,128,128]{2,1,0:T(8,128)(2,1)S(1)} %bitcast.6, f32[8,1,256]{2,1,0:T(1,128)S(1)} %get-tuple-element.5.lse_ref), custom_call_target="tpu_custom_call" | custom-call | tf_op jit(solution)/shard_map/place/pallas_call | solution.py:421

commit v5 on v4

--- a/solution.py
+++ b/solution.py
@@ -200,64 +200,55 @@
             sbuf[e][pl.ds(cache, tok), :] = st
             mbuf[e][...] = fold_max(mx, st)
 
-    def wait_inputs(i):
+    def region(i, sc, sn, mc, mn):
+        nxt = lax.rem(i + 1, n_pairs)
+        f_n, slot_n, kv_n, owner_n, home_n = pair(nxt)
         _, slot, kv, _, _ = pair(i)
-
-        @pl.when(among(i, Q_PAIRS))
+        later = jnp.minimum(i + 2, n_pairs - 1)
+        ahead = pair(later)[1]
+
+        @pl.when(among(i + 2, Q_PAIRS))
         def _():
             for e in range(2):
-                pltpu.make_async_copy(qraw.at[slot + e], qraw.at[slot + e], q_recv.at[slot + e]).wait()
-
-    def wait_kv(i):
-        _, slot, kv, _, _ = pair(i)
-
-        @pl.when(among(i, KV_PAIRS))
+                pltpu.make_async_copy(qraw.at[ahead + e], qraw.at[ahead + e], q_recv.at[ahead + e]).wait()
+
+        @pl.when(among(i + 1, KV_PAIRS))
         def _():
             for e in range(2):
-                pltpu.make_async_copy(kbuf.at[kv + e], kbuf.at[kv + e], k_recv.at[kv + e - kvh]).wait()
-                pltpu.make_async_copy(vbuf.at[kv + e], vbuf.at[kv + e], v_recv.at[kv + e - kvh]).wait()
-
-    def region(r):
-        cur = [2 * r, 2 * r + 1, jnp.minimum(2 * r + 2, n_pairs - 1), jnp.minimum(2 * r + 3, n_pairs - 1)]
-        wait_inputs(2 * r + 2)
-        wait_inputs(2 * r + 3)
-        wait_kv(2 * r + 1)
-        wait_kv(2 * r + 2)
-        info = [pair(c) for c in cur]
-        units = [tuple(x + e if k in (1, 2) else x for k, x in enumerate(info[p])) for p in range(3) for e in range(2)]
+                pltpu.make_async_copy(kbuf.at[kv_n + e], kbuf.at[kv_n + e], k_recv.at[kv_n + e - kvh]).wait()
+                pltpu.make_async_copy(vbuf.at[kv_n + e], vbuf.at[kv_n + e], v_recv.at[kv_n + e - kvh]).wait()
+
+        qv, m, decay, mx, l8, o = [], [], [], [None] * 2, [], [None] * 2
         for e in range(2):
-            load_q(info[2][1] + e)
-        m_old = [st_m[units[e][1]] for e in range(4)]
-        for e in range(4):
-            _, slot, kv, _, _ = units[e]
-            f_n, slot_n, kv_n, owner_n, home_n = units[e + 2]
-            n = (e + 2) % 4
-            qv = qt[slot_n]
-            m = jnp.maximum(m_old[e], jnp.max(mbuf[e][...], axis=0, keepdims=True) * scale2)
-            decay = jnp.exp2(m_old[e] - m)
-            mx, o, l8 = None, None, jnp.zeros((8, rows), F32)
-            for c in range(chunks):
-                sl = pl.ds(c * TK, TK)
-                st = qk_tile(kv_n, f_n, c, qv)
-                p = jnp.exp2(sbuf[e][sl, :] * scale2 - m)
-                sbuf[n][sl, :] = st
-                mx = fold_max(mx, st)
-                l8 = l8 + jnp.sum(p.reshape(TK // 8, 8, rows), axis=0)
-                t = jnp.dot(vbuf[kv, :, sl], p.astype(BF), preferred_element_type=F32)
-                o = t if o is None else o + t
-            sl = pl.ds(cache, tok)
-            st = qk_new(kv_n, owner_n, home_n, qv)
-            p = jnp.exp2(sbuf[e][sl, :] * scale2 - m)
-            sbuf[n][sl, :] = st
-            mbuf[n][...] = fold_max(mx, st)
-            l8 = l8 + jnp.sum(p.reshape(tok // 8, 8, rows), axis=0)
+            qv.append(qt[slot_n + e])
+            m_old = st_m[slot + e]
+            m.append(jnp.maximum(m_old, jnp.max(mc[e][...], axis=0, keepdims=True) * scale2))
+            decay.append(jnp.exp2(m_old - m[e]))
+            l8.append(jnp.zeros((8, rows), F32))
+        for c in range(chunks):
+            sl = pl.ds(c * TK, TK)
+            for e in range(2):
+                st = qk_tile(kv_n + e, f_n, c, qv[e])
+                p = jnp.exp2(sc[e][sl, :] * scale2 - m[e])
+                sn[e][sl, :] = st
+                mx[e] = fold_max(mx[e], st)
+                l8[e] = l8[e] + jnp.sum(p.reshape(TK // 8, 8, rows), axis=0)
+                t = jnp.dot(vbuf[kv + e, :, sl], p.astype(BF), preferred_element_type=F32)
+                o[e] = t if o[e] is None else o[e] + t
+        sl = pl.ds(cache, tok)
+        for e in range(2):
+            st = qk_new(kv_n + e, owner_n, home_n, qv[e])
+            p = jnp.exp2(sc[e][sl, :] * scale2 - m[e])
+            sn[e][sl, :] = st
+            mn[e][...] = fold_max(mx[e], st)
+            l8[e] = l8[e] + jnp.sum(p.reshape(tok // 8, 8, rows), axis=0)
             pb = jnp.concatenate([p.astype(BF), jnp.zeros((dim - tok, rows), BF)], axis=0)
-            o = o + jnp.dot(vbuf[kv, :, pl.ds(cache, dim)], pb, preferred_element_type=F32)
-            st_o[slot] = st_o[slot] * decay + o
-            st_l[slot] = st_l[slot] * decay + jnp.sum(l8, axis=0, keepdims=True)
-            st_m[slot] = m
+            o[e] = o[e] + jnp.dot(vbuf[kv + e, :, pl.ds(cache, dim)], pb, preferred_element_type=F32)
         for e in range(2):
-            load_q(info[3][1] + e)
+            st_o[slot + e] = st_o[slot + e] * decay[e] + o[e]
+            st_l[slot + e] = st_l[slot + e] * decay[e] + jnp.sum(l8[e], axis=0, keepdims=True)
+            st_m[slot + e] = m[e]
+            load_q(ahead + e)
 
     def partial_copies(u):
         return (pltpu.make_async_remote_copy(
@@ -329,10 +320,11 @@
     kv_start(cache - raw_pos, raw_pos)
 
     @pl.loop(0, n_pairs // 2)
-    def _(r):
-        region(r)
-        finish(2 * r)
-        finish(2 * r + 1)
+    def _(i):
+        region(2 * i, sbuf[:2], sbuf[2:], mbuf[:2], mbuf[2:])
+        finish(2 * i)
+        region(2 * i + 1, sbuf[2:], sbuf[:2], mbuf[2:], mbuf[:2])
+        finish(2 * i + 1)
 
     for k in range(3):
         for h in range(half):

time: 46.4 us -> 39.6 us (0.85)
  Pallas kernels: 45 us -> 38.2 us
    pallas_call x1, Pallas kernels: 44.2 us -> 37.4 us  [local(): pl.pallas_call(attend_kernel, out_shape=(pltpu.VMEM((tok, kvh, ratio, dim...]
where the time goes in v5:
time: 39.6 us; the launch traced here: 39.5 us
  Pallas kernels  38.2 us (96%)
  between operations  1.29 us (3%)
    pallas_call x1, Pallas kernels, local(): pl.pallas_call(attend_kernel, out_shape=(pltpu.VMEM((tok, kvh, ratio, dim...  37.4 us
    pallas_call x1, Pallas kernels, local(): pl.pallas_call(place_kernel, out_shape=(jax.ShapeDtypeStruct((tok, heads,...  0.82 us

profile of v5, /device:TPU:0, one launch (start us, length us, event | category | flops | bytes accessed | tf_op | source)
XLA Modules:
  0.0 39.5 jit_solution(10457464719381181106)
XLA Ops:
  1.3 37.4 %attend.1 = (bf16[16,8,16,128]{3,2,1,0:T(8,128)(2,1)S(1)}, f32[8,1,256]{2,1,0:T(1,128)S(1)}) custom-call(bf16[16,8,16,128]{3,2,1,0:T(8,128)(2,1)} %bitcast.9, bf16[128,128]{1,0:T(8,128)(2,1)} %bitcast.10, bf16[128,128]{1,0:T(8,128)(2,1)} %bitcast.11, bf16[24576,128]{1,0:T(8,128)(2,1)} %bitcast.7, bf16[24576,128]{1,0:T(8,128)(2,1)} %bitcast.8, s32[1]{0:T(128)S(6)} %copy.8.plen_ref), custom_call_target="tpu_custom_call" | custom-call | flops 12884901888 | bytes 12582912 | tf_op jit(solution)/shard_map/attend/pallas_call | solution.py:402
  38.7 0.8 %place.1 = (bf16[16,128,128]{2,1,0:T(8,128)(2,1)}, f32[16,128]{1,0:T(8,128)}) custom-call(bf16[16,128,128]{2,1,0:T(8,128)(2,1)S(1)} %bitcast.6, f32[8,1,256]{2,1,0:T(1,128)S(1)} %get-tuple-element.5.lse_ref), custom_call_target="tpu_custom_call" | custom-call | tf_op jit(solution)/shard_map/place/pallas_call | solution.py:413

commit v6 on v5

--- a/solution.py
+++ b/solution.py
@@ -11,7 +11,6 @@
 MESH = pl.DeviceIdType.MESH
 BIG = 1e30
 TK = 256
-PREP = 128
 BF = jnp.bfloat16
 SEQ = ((0, 0), (2, 0), (4, 0), (12, 0), (14, 0), (12, 1), (8, 0), (14, 1),
        (10, 0), (8, 1), (10, 1), (6, 0), (4, 1), (6, 1), (0, 1), (2, 1))
@@ -37,8 +36,8 @@
     return hit
 
 
-def attend_kernel(q_hbm, kn_hbm, vn_hbm, kc_hbm, vc_hbm, plen_ref, out_ref, lse_ref,
-                  raw_k, raw_v, new_k, new_v, kbuf, vbuf, bias, qraw, qt, sbuf, mbuf,
+def attend_kernel(q_hbm, kn_hbm, vn_hbm, kc_hbm, vc_hbm, plen_hbm, out_ref, lse_ref,
+                  raw_k, raw_v, new_k, new_v, kbuf, vbuf, bias, qraw, qt, pick, plen, sbuf, mbuf,
                   st_o, st_m, st_l, ps, psl, pr, prl, fo, fl,
                   raw_sem, new_sem, q_send, q_recv, kv_send, k_recv, v_recv, p_send, p_recv, f_send, f_recv):
     tok, kvh, ratio, dim = q_hbm.shape
@@ -69,6 +68,8 @@
         a, b = raw_copy(j)
         a.start()
         b.start()
+    plen_copy = pltpu.make_async_copy(plen_hbm, plen, new_sem.at[2])
+    plen_copy.start()
     new_copies = (pltpu.make_async_copy(kn_hbm, new_k, new_sem.at[0]),
                   pltpu.make_async_copy(vn_hbm, new_v, new_sem.at[1]))
     for cp in new_copies:
@@ -80,14 +81,9 @@
     for peer in (mate, far, far_other):
         pl.semaphore_signal(barrier, inc=1, device_id={'cp': peer}, device_id_type=MESH)
 
-    ones_row = jnp.where(lax.broadcasted_iota(jnp.int32, (dim, rows), 0) == 0, 1.0, 0.0).astype(BF)
-
-    @pl.loop(0, 4 * half)
-    def _(j):
-        qt[j, pl.ds(dim, dim), :] = ones_row
-        st_o[j] = jnp.zeros((dim, rows), F32)
-        st_m[j] = jnp.full((1, rows), -1e38, F32)
-        st_l[j] = jnp.zeros((1, rows), F32)
+    pick[...] = jnp.where(lax.broadcasted_iota(jnp.int32, (dim, rows), 0) == 0, 1.0, 0.0).astype(BF)
+    for e in range(2):
+        mbuf[e][...] = jnp.full((8, rows), -3e38, F32)
 
     pl.semaphore_wait(barrier, 3)
 
@@ -103,7 +99,8 @@
         for h in range(half):
             q_copy(k, h).start()
 
-    visible_len = plen_ref[0]
+    plen_copy.wait()
+    visible_len = plen[0]
     for f, owner in enumerate((me, mate)):
         @pl.loop(0, chunks)
         def _(j):
@@ -123,7 +120,7 @@
     def kv_parts(h, lo, n):
         src = half * (1 - core) + h
         to = dict(device_id={'cp': mate}, device_id_type=MESH)
-        k_rows, v_lanes = pl.ds(lo, min(n, cache + tok - lo)), pl.ds(lo, n)
+        k_rows, v_lanes = pl.ds(lo, tok if n == dim else n), pl.ds(lo, n)
         return (pltpu.make_async_remote_copy(
                     src_ref=kbuf.at[src, k_rows], dst_ref=kbuf.at[kvh + h, k_rows],
                     send_sem=kv_send.at[0, h], recv_sem=k_recv.at[h], **to),
@@ -135,25 +132,6 @@
         for h in range(half):
             for cp in kv_parts(h, lo, n):
                 cp.start()
-
-    for j in range(n_raw):
-        for cp in raw_copy(j):
-            cp.wait()
-
-        @pl.loop(0, raw_pos // PREP)
-        def _(i):
-            base = pl.multiple_of(j * raw_pos + i * PREP, PREP)
-            src = pl.ds(pl.multiple_of(base * kvh, PREP * kvh), PREP * kvh)
-            xk = pltpu.einshape('phd->hpd', raw_k[src, :].reshape(PREP, kvh, dim))
-            xv = pltpu.einshape('phd->hpd', raw_v[src, :].reshape(PREP, kvh, dim))
-            for h in range(kvh):
-                kbuf[h, pl.ds(base, PREP), :] = xk[h]
-                vbuf[h, :, pl.ds(base, PREP)] = xv[h].T
-
-        if j == 0:
-            kv_start(cache, dim)
-        else:
-            kv_start((j - 1) * raw_pos, raw_pos)
 
     n_pairs = 4 * half
 
@@ -169,10 +147,13 @@
         return second, slot, kv, owner, home
 
     def load_q(slot):
-        qt[slot, pl.ds(0, dim), :] = qraw[slot].reshape(rows, dim).T
+        qt[slot] = qraw[slot].reshape(rows, dim).T
+
+    def score_rhs(slot):
+        return jnp.concatenate([qt[slot], pick[...]], axis=0)
 
     def qk_tile(kv, f, c, qv):
-        sl = pl.ds(c * TK, TK)
+        sl = pl.ds(c * TK if isinstance(c, int) else pl.multiple_of(c * TK, TK), TK)
         lhs = jnp.concatenate([kbuf[kv, sl, :], bias[f, sl, :]], axis=1)
         return jnp.dot(lhs, qv, preferred_element_type=F32)
 
@@ -187,23 +168,60 @@
         t = jnp.max(st.reshape(st.shape[0] // 8, 8, rows), axis=0)
         return t if mx is None else jnp.maximum(mx, t)
 
-    def first_scores():
-        f, slot, kv, owner, home = pair(0)
+    def prepare(c):
+        base = pl.multiple_of(c * TK, TK)
+        src = pl.ds(pl.multiple_of(base * kvh, TK * kvh), TK * kvh)
+        xk = pltpu.einshape('phd->hpd', raw_k[src, :].reshape(TK, kvh, dim))
+        xv = pltpu.einshape('phd->hpd', raw_v[src, :].reshape(TK, kvh, dim))
+        for h in range(kvh):
+            kbuf[h, pl.ds(base, TK), :] = xk[h]
+            vbuf[h, :, pl.ds(base, TK)] = xv[h].T
+
+    f_0, slot_0, kv_0, owner_0, home_0 = pair(0)
+
+    def first_scores(c):
         for e in range(2):
-            qv = qt[slot + e]
-            mx = None
-            for c in range(chunks):
-                st = qk_tile(kv + e, f, c, qv)
-                sbuf[e][pl.ds(c * TK, TK), :] = st
-                mx = fold_max(mx, st)
-            st = qk_new(kv + e, owner, home, qv)
-            sbuf[e][pl.ds(cache, tok), :] = st
-            mbuf[e][...] = fold_max(mx, st)
-
-    def region(i, sc, sn, mc, mn):
+            st = qk_tile(kv_0 + e, f_0, c, score_rhs(slot_0 + e))
+            sbuf[e][pl.ds(pl.multiple_of(c * TK, TK), TK), :] = st
+            mbuf[e][...] = fold_max(mbuf[e][...], st)
+
+    per_raw = raw_pos // TK
+    for h in range(half):
+        own_q(h).wait()
+    for h in range(half):
+        load_q(h)
+    for cp in raw_copy(0):
+        cp.wait()
+    kv_start(cache, dim)
+    prepare(0)
+
+    @pl.loop(1, chunks)
+    def _(c):
+        @pl.when(lax.rem(c, per_raw) == 0)
+        def _():
+            j = lax.div(c, per_raw)
+            for cp in raw_copy(j):
+                cp.wait()
+
+            @pl.when(j >= 2)
+            def _():
+                kv_start(pl.multiple_of((j - 2) * raw_pos, raw_pos), raw_pos)
+
+        first_scores(c - 1)
+        prepare(c)
+
+    kv_start(cache - 2 * raw_pos, raw_pos)
+    first_scores(chunks - 1)
+    for e in range(2):
+        st = qk_new(kv_0 + e, owner_0, home_0, score_rhs(slot_0 + e))
+        sbuf[e][pl.ds(cache, tok), :] = st
+        mbuf[e][...] = fold_max(mbuf[e][...], st)
+    kv_start(cache - raw_pos, raw_pos)
+
+    def region(i, sc, sn, mc, mn, more=True):
         nxt = lax.rem(i + 1, n_pairs)
         f_n, slot_n, kv_n, owner_n, home_n = pair(nxt)
-        _, slot, kv, _, _ = pair(i)
+        second, slot, kv, _, _ = pair(i)
         later = jnp.minimum(i + 2, n_pairs - 1)
         ahead = pair(later)[1]
 
@@ -220,35 +238,38 @@
 
         qv, m, decay, mx, l8, o = [], [], [], [None] * 2, [], [None] * 2
         for e in range(2):
-            qv.append(qt[slot_n + e])
-            m_old = st_m[slot + e]
+            qv.append(score_rhs(slot_n + e) if more else None)
+            m_old = jnp.where(second == 1, st_m[slot + e], -1e38)
             m.append(jnp.maximum(m_old, jnp.max(mc[e][...], axis=0, keepdims=True) * scale2))
             decay.append(jnp.exp2(m_old - m[e]))
             l8.append(jnp.zeros((8, rows), F32))
         for c in range(chunks):
             sl = pl.ds(c * TK, TK)
             for e in range(2):
-                st = qk_tile(kv_n + e, f_n, c, qv[e])
+                st = qk_tile(kv_n + e, f_n, c, qv[e]) if more else None
                 p = jnp.exp2(sc[e][sl, :] * scale2 - m[e])
-                sn[e][sl, :] = st
-                mx[e] = fold_max(mx[e], st)
+                if more:
+                    sn[e][sl, :] = st
+                    mx[e] = fold_max(mx[e], st)
                 l8[e] = l8[e] + jnp.sum(p.reshape(TK // 8, 8, rows), axis=0)
                 t = jnp.dot(vbuf[kv + e, :, sl], p.astype(BF), preferred_element_type=F32)
                 o[e] = t if o[e] is None else o[e] + t
         sl = pl.ds(cache, tok)
         for e in range(2):
-            st = qk_new(kv_n + e, owner_n, home_n, qv[e])
             p = jnp.exp2(sc[e][sl, :] * scale2 - m[e])
-            sn[e][sl, :] = st
-            mn[e][...] = fold_max(mx[e], st)
+            if more:
+                st = qk_new(kv_n + e, owner_n, home_n, qv[e])
+                sn[e][sl, :] = st
+                mn[e][...] = fold_max(mx[e], st)
             l8[e] = l8[e] + jnp.sum(p.reshape(tok // 8, 8, rows), axis=0)
             pb = jnp.concatenate([p.astype(BF), jnp.zeros((dim - tok, rows), BF)], axis=0)
             o[e] = o[e] + jnp.dot(vbuf[kv + e, :, pl.ds(cache, dim)], pb, preferred_element_type=F32)
         for e in range(2):
-            st_o[slot + e] = st_o[slot + e] * decay[e] + o[e]
-            st_l[slot + e] = st_l[slot + e] * decay[e] + jnp.sum(l8[e], axis=0, keepdims=True)
+            st_o[slot + e] = jnp.where(second == 1, st_o[slot + e] * decay[e], 0.0) + o[e]
+            st_l[slot + e] = jnp.where(second == 1, st_l[slot + e] * decay[e], 0.0) + jnp.sum(l8[e], axis=0, keepdims=True)
             st_m[slot + e] = m[e]
-            load_q(ahead + e)
+            if more:
+                load_q(ahead + e)
 
     def partial_copies(u):
         return (pltpu.make_async_remote_copy(
@@ -312,19 +333,17 @@
                     for cp in mate_out(u + e):
                         cp.start()
 
-    for h in range(half):
-        own_q(h).wait()
-    for h in range(half):
-        load_q(h)
-    first_scores()
-    kv_start(cache - raw_pos, raw_pos)
-
-    @pl.loop(0, n_pairs // 2)
-    def _(i):
+    def two(i, more):
         region(2 * i, sbuf[:2], sbuf[2:], mbuf[:2], mbuf[2:])
         finish(2 * i)
-        region(2 * i + 1, sbuf[2:], sbuf[:2], mbuf[2:], mbuf[:2])
+        region(2 * i + 1, sbuf[2:], sbuf[:2], mbuf[2:], mbuf[:2], more)
         finish(2 * i + 1)
+
+    @pl.loop(0, n_pairs // 2 - 1)
+    def _(i):
+        two(i, True)
+
+    two(jnp.int32(n_pairs // 2 - 1), False)
 
     for k in range(3):
         for h in range(half):
@@ -383,7 +402,9 @@
             pltpu.VMEM((kvh + half, dim, cache + dim), BF),
             pltpu.VMEM((2, cache, dim), BF),
             pltpu.VMEM((4 * half, tok, ratio, dim), BF),
-            pltpu.VMEM((4 * half, 2 * dim, rows), BF),
+            pltpu.VMEM((4 * half, dim, rows), BF),
+            pltpu.VMEM((dim, rows), BF),
+            pltpu.SMEM((1,), jnp.int32),
             (pltpu.VMEM((cache + tok, rows), F32),) * 4,
             (pltpu.VMEM((8, rows), F32),) * 4,
             pltpu.VMEM((4 * half, dim, rows), F32),
@@ -395,14 +416,14 @@
             pltpu.VMEM((2 * half, 1, rows), F32),
             pltpu.VMEM((half, tok, ratio, dim), BF),
             pltpu.VMEM((half, 1, rows), F32),
-            dma((2, n_raw)), dma((2,)), dma((3 * half,)), dma((4 * half,)), dma((2, half)), dma((half,)), dma((half,)),
+            dma((2, n_raw)), dma((3,)), dma((3 * half,)), dma((4 * half,)), dma((2, half)), dma((half,)), dma((half,)),
             dma((2, 2 * half)), dma((2, 2 * half)), dma((2, half)), dma((2, half)),
         ]
         flops = 4 * heads * tok * 4 * cache * dim
         out, lse = pl.pallas_call(
             attend_kernel,
             out_shape=(pltpu.VMEM((tok, kvh, ratio, dim), BF), pltpu.VMEM((kvh, 1, rows), F32)),
-            in_specs=[hbm] * 5 + [pl.BlockSpec(memory_space=pltpu.SMEM)],
+            in_specs=[hbm] * 6,
             out_specs=(vmem, vmem),
             scratch_shapes=scratch,
             compiler_params=pltpu.CompilerParams(collective_id=0, has_side_effects=True, vmem_limit_bytes=60 * 2 ** 20),

time: 39.6 us -> 40.6 us (1.025)
  Pallas kernels: 38.2 us -> 39.2 us
    pallas_call x1, Pallas kernels: 37.4 us -> 38.4 us  [local(): pl.pallas_call(attend_kernel, out_shape=(pltpu.VMEM((tok, kvh, ratio, dim...]
where the time goes in v6:
time: 40.6 us; the launch traced here: 40.5 us
  Pallas kernels  39.2 us (97%)
  between operations  1.29 us (3%)
    pallas_call x1, Pallas kernels, local(): pl.pallas_call(attend_kernel, out_shape=(pltpu.VMEM((tok, kvh, ratio, dim...  38.4 us
    pallas_call x1, Pallas kernels, local(): pl.pallas_call(place_kernel, out_shape=(jax.ShapeDtypeStruct((tok, heads,...  0.82 us

profile of v6, /device:TPU:0, one launch (start us, length us, event | category | flops | bytes accessed | tf_op | source)
XLA Modules:
  0.0 40.5 jit_solution(15554966158991993337)
XLA Ops:
  1.3 38.4 %attend.1 = (bf16[16,8,16,128]{3,2,1,0:T(8,128)(2,1)S(1)}, f32[8,1,256]{2,1,0:T(1,128)S(1)}) custom-call(bf16[16,8,16,128]{3,2,1,0:T(8,128)(2,1)} %bitcast.9, bf16[128,128]{1,0:T(8,128)(2,1)} %bitcast.10, bf16[128,128]{1,0:T(8,128)(2,1)} %bitcast.11, bf16[24576,128]{1,0:T(8,128)(2,1)} %bitcast.7, bf16[24576,128]{1,0:T(8,128)(2,1)} %bitcast.8, s32[1]{0:T(128)S(6)} %copy.8.plen_hbm), custom_call_target="tpu_custom_call" | custom-call | flops 12884901888 | bytes 12582912 | tf_op jit(solution)/shard_map/attend/pallas_call | solution.py:423
  39.7 0.8 %place.1 = (bf16[16,128,128]{2,1,0:T(8,128)(2,1)}, f32[16,128]{1,0:T(8,128)}) custom-call(bf16[16,128,128]{2,1,0:T(8,128)(2,1)S(1)} %bitcast.6, f32[8,1,256]{2,1,0:T(1,128)S(1)} %get-tuple-element.5.lse_ref), custom_call_target="tpu_custom_call" | custom-call | tf_op jit(solution)/shard_map/place/pallas_call | solution.py:434

commit v7 on v6

--- a/solution.py
+++ b/solution.py
@@ -12,8 +12,8 @@
 BIG = 1e30
 TK = 256
 BF = jnp.bfloat16
-SEQ = ((0, 0), (2, 0), (4, 0), (12, 0), (14, 0), (12, 1), (8, 0), (14, 1),
-       (10, 0), (8, 1), (10, 1), (6, 0), (4, 1), (6, 1), (0, 1), (2, 1))
+SEQ = ((0, 0), (2, 0), (4, 0), (12, 0), (14, 0), (8, 0), (12, 1), (10, 0),
+       (14, 1), (8, 1), (10, 1), (6, 0), (4, 1), (6, 1), (0, 1), (2, 1))
 F32 = jnp.float32
 
 

time: 40.6 us -> 41.8 us (1.030)
  Pallas kernels: 39.2 us -> 40.4 us
    pallas_call x1, Pallas kernels: 38.4 us -> 39.6 us  [local(): pl.pallas_call(attend_kernel, out_shape=(pltpu.VMEM((tok, kvh, ratio, dim...]
where the time goes in v7:
time: 41.8 us; the launch traced here: 41.7 us
  Pallas kernels  40.4 us (97%)
  between operations  1.29 us (3%)
    pallas_call x1, Pallas kernels, local(): pl.pallas_call(attend_kernel, out_shape=(pltpu.VMEM((tok, kvh, ratio, dim...  39.6 us

profile of v7, /device:TPU:0, one launch (start us, length us, event | category | flops | bytes accessed | tf_op | source)
XLA Modules:
  0.0 41.7 jit_solution(7120387971204810419)
XLA Ops:
  1.3 39.6 %attend.1 = (bf16[16,8,16,128]{3,2,1,0:T(8,128)(2,1)S(1)}, f32[8,1,256]{2,1,0:T(1,128)S(1)}) custom-call(bf16[16,8,16,128]{3,2,1,0:T(8,128)(2,1)} %bitcast.9, bf16[128,128]{1,0:T(8,128)(2,1)} %bitcast.10, bf16[128,128]{1,0:T(8,128)(2,1)} %bitcast.11, bf16[24576,128]{1,0:T(8,128)(2,1)} %bitcast.7, bf16[24576,128]{1,0:T(8,128)(2,1)} %bitcast.8, s32[1]{0:T(128)S(6)} %copy.8.plen_hbm), custom_call_target="tpu_custom_call" | custom-call | flops 12884901888 | bytes 12582912 | tf_op jit(solution)/shard_map/attend/pallas_call | solution.py:423
  40.9 0.8 %place.1 = (bf16[16,128,128]{2,1,0:T(8,128)(2,1)}, f32[16,128]{1,0:T(8,128)}) custom-call(bf16[16,128,128]{2,1,0:T(8,128)(2,1)S(1)} %bitcast.6, f32[8,1,256]{2,1,0:T(1,128)S(1)} %get-tuple-element.5.lse_ref), custom_call_target="tpu_custom_call" | custom-call | tf_op jit(solution)/shard_map/place/pallas_call | solution.py:434

commit v8 on v6

--- a/solution.py
+++ b/solution.py
@@ -11,6 +11,7 @@
 MESH = pl.DeviceIdType.MESH
 BIG = 1e30
 TK = 256
+PREP = 128
 BF = jnp.bfloat16
 SEQ = ((0, 0), (2, 0), (4, 0), (12, 0), (14, 0), (12, 1), (8, 0), (14, 1),
        (10, 0), (8, 1), (10, 1), (6, 0), (4, 1), (6, 1), (0, 1), (2, 1))
@@ -168,50 +169,39 @@
         t = jnp.max(st.reshape(st.shape[0] // 8, 8, rows), axis=0)
         return t if mx is None else jnp.maximum(mx, t)
 
-    def prepare(c):
-        base = pl.multiple_of(c * TK, TK)
-        src = pl.ds(pl.multiple_of(base * kvh, TK * kvh), TK * kvh)
-        xk = pltpu.einshape('phd->hpd', raw_k[src, :].reshape(TK, kvh, dim))
-        xv = pltpu.einshape('phd->hpd', raw_v[src, :].reshape(TK, kvh, dim))
-        for h in range(kvh):
-            kbuf[h, pl.ds(base, TK), :] = xk[h]
-            vbuf[h, :, pl.ds(base, TK)] = xv[h].T
-
     f_0, slot_0, kv_0, owner_0, home_0 = pair(0)
 
     def first_scores(c):
         for e in range(2):
             st = qk_tile(kv_0 + e, f_0, c, score_rhs(slot_0 + e))
-            sbuf[e][pl.ds(pl.multiple_of(c * TK, TK), TK), :] = st
+            sbuf[e][pl.ds(c * TK, TK), :] = st
             mbuf[e][...] = fold_max(mbuf[e][...], st)
 
-    per_raw = raw_pos // TK
+    for j in range(n_raw):
+        for cp in raw_copy(j):
+            cp.wait()
+
+        @pl.loop(0, raw_pos // PREP)
+        def _(i):
+            base = pl.multiple_of(j * raw_pos + i * PREP, PREP)
+            src = pl.ds(pl.multiple_of(base * kvh, PREP * kvh), PREP * kvh)
+            xk = pltpu.einshape('phd->hpd', raw_k[src, :].reshape(PREP, kvh, dim))
+            xv = pltpu.einshape('phd->hpd', raw_v[src, :].reshape(PREP, kvh, dim))
+            for h in range(kvh):
+                kbuf[h, pl.ds(base, PREP), :] = xk[h]
+                vbuf[h, :, pl.ds(base, PREP)] = xv[h].T
+
+        if j == 0:
+            kv_start(cache, dim)
+        else:
+            kv_start((j - 1) * raw_pos, raw_pos)
+
     for h in range(half):
         own_q(h).wait()
     for h in range(half):
         load_q(h)
-    for cp in raw_copy(0):
-        cp.wait()
-    kv_start(cache, dim)
-    prepare(0)
-
-    @pl.loop(1, chunks)
-    def _(c):
-        @pl.when(lax.rem(c, per_raw) == 0)
-        def _():
-            j = lax.div(c, per_raw)
-            for cp in raw_copy(j):
-                cp.wait()
-
-            @pl.when(j >= 2)
-            def _():
-                kv_start(pl.multiple_of((j - 2) * raw_pos, raw_pos), raw_pos)
-
-        first_scores(c - 1)
-        prepare(c)
-
-    kv_start(cache - 2 * raw_pos, raw_pos)
-    first_scores(chunks - 1)
+    for c in range(chunks):
+        first_scores(c)
     for e in range(2):
         st = qk_new(kv_0 + e, owner_0, home_0, score_rhs(slot_0 + e))
         sbuf[e][pl.ds(cache, tok), :] = st

time: 40.6 us -> 39.6 us (0.975)
  Pallas kernels: 39.2 us -> 38.2 us
    pallas_call x1, Pallas kernels: 38.4 us -> 37.4 us  [local(): pl.pallas_call(attend_kernel, out_shape=(pltpu.VMEM((tok, kvh, ratio, dim...]
where the time goes in v8:
time: 39.6 us; the launch traced here: 39.5 us
  Pallas kernels  38.2 us (96%)
  between operations  1.29 us (3%)
    pallas_call x1, Pallas kernels, local(): pl.pallas_call(attend_kernel, out_shape=(pltpu.VMEM((tok, kvh, ratio, dim...  37.4 us
    pallas_call x1, Pallas kernels, local(): pl.pallas_call(place_kernel, out_shape=(jax.ShapeDtypeStruct((tok, heads,...  0.82 us

profile of v8, /device:TPU:0, one launch (start us, length us, event | category | flops | bytes accessed | tf_op | source)
XLA Modules:
  0.0 39.5 jit_solution(15166436556332925289)
XLA Ops:
  1.3 37.4 %attend.1 = (bf16[16,8,16,128]{3,2,1,0:T(8,128)(2,1)S(1)}, f32[8,1,256]{2,1,0:T(1,128)S(1)}) custom-call(bf16[16,8,16,128]{3,2,1,0:T(8,128)(2,1)} %bitcast.9, bf16[128,128]{1,0:T(8,128)(2,1)} %bitcast.10, bf16[128,128]{1,0:T(8,128)(2,1)} %bitcast.11, bf16[24576,128]{1,0:T(8,128)(2,1)} %bitcast.7, bf16[24576,128]{1,0:T(8,128)(2,1)} %bitcast.8, s32[1]{0:T(128)S(6)} %copy.8.plen_hbm), custom_call_target="tpu_custom_call" | custom-call | flops 12884901888 | bytes 12582912 | tf_op jit(solution)/shard_map/attend/pallas_call | solution.py:413
  38.7 0.8 %place.1 = (bf16[16,128,128]{2,1,0:T(8,128)(2,1)}, f32[16,128]{1,0:T(8,128)}) custom-call(bf16[16,128,128]{2,1,0:T(8,128)(2,1)S(1)} %bitcast.6, f32[8,1,256]{2,1,0:T(1,128)S(1)} %get-tuple-element.5.lse_ref), custom_call_target="tpu_custom_call" | custom-call | tf_op jit(solution)/shard_map/place/pallas_call | solution.py:424

commit v9 on v8

--- a/solution.py
+++ b/solution.py
@@ -12,6 +12,7 @@
 BIG = 1e30
 TK = 256
 PREP = 128
+RAW_DEPTH = 3
 BF = jnp.bfloat16
 SEQ = ((0, 0), (2, 0), (4, 0), (12, 0), (14, 0), (12, 1), (8, 0), (14, 1),
        (10, 0), (8, 1), (10, 1), (6, 0), (4, 1), (6, 1), (0, 1), (2, 1))
@@ -65,10 +66,12 @@
     def own_q(h):
         return pltpu.make_async_copy(q_hbm.at[:, half * core + h], qraw.at[h], q_recv.at[h])
 
-    for j in range(n_raw):
-        a, b = raw_copy(j)
-        a.start()
-        b.start()
+    def raw_start(j):
+        for cp in raw_copy(j):
+            cp.start()
+
+    for j in range(RAW_DEPTH):
+        raw_start(j)
     plen_copy = pltpu.make_async_copy(plen_hbm, plen, new_sem.at[2])
     plen_copy.start()
     new_copies = (pltpu.make_async_copy(kn_hbm, new_k, new_sem.at[0]),
@@ -180,6 +183,8 @@
     for j in range(n_raw):
         for cp in raw_copy(j):
             cp.wait()
+        if j + RAW_DEPTH < n_raw:
+            raw_start(j + RAW_DEPTH)
 
         @pl.loop(0, raw_pos // PREP)
         def _(i):
@@ -193,8 +198,8 @@
 
         if j == 0:
             kv_start(cache, dim)
-        else:
-            kv_start((j - 1) * raw_pos, raw_pos)
+        if j % 2 and j > 1:
+            kv_start((j - 3) * raw_pos, 2 * raw_pos)
 
     for h in range(half):
         own_q(h).wait()
@@ -206,7 +211,7 @@
         st = qk_new(kv_0 + e, owner_0, home_0, score_rhs(slot_0 + e))
         sbuf[e][pl.ds(cache, tok), :] = st
         mbuf[e][...] = fold_max(mbuf[e][...], st)
-    kv_start(cache - raw_pos, raw_pos)
+    kv_start(cache - 2 * raw_pos, 2 * raw_pos)
 
     def region(i, sc, sn, mc, mn, more=True):
         nxt = lax.rem(i + 1, n_pairs)
@@ -379,7 +384,7 @@
         ratio = heads // kvh
         half = kvh // 2
         rows = tok * ratio
-        n_raw = 6
+        n_raw = cache // TK
         dma = pltpu.SemaphoreType.DMA
         hbm = pl.BlockSpec(memory_space=pltpu.HBM)
         vmem = pl.BlockSpec(memory_space=pltpu.VMEM)

time: 39.6 us -> 39.7 us (level)
  no operation moved by 1% of the time
where the time goes in v9:
time: 39.7 us; the launch traced here: 39.6 us
  Pallas kernels  38.3 us (96%)
  between operations  1.29 us (3%)
    pallas_call x1, Pallas kernels, local(): pl.pallas_call(attend_kernel, out_shape=(pltpu.VMEM((tok, kvh, ratio, dim...  37.5 us
    pallas_call x1, Pallas kernels, local(): pl.pallas_call(place_kernel, out_shape=(jax.ShapeDtypeStruct((tok, heads,...  0.82 us

profile of v9, /device:TPU:0, one launch (start us, length us, event | category | flops | bytes accessed | tf_op | source)
XLA Modules:
  0.0 39.6 jit_solution(5337294538522345807)
XLA Ops:
  1.3 37.5 %attend.1 = (bf16[16,8,16,128]{3,2,1,0:T(8,128)(2,1)S(1)}, f32[8,1,256]{2,1,0:T(1,128)S(1)}) custom-call(bf16[16,8,16,128]{3,2,1,0:T(8,128)(2,1)} %bitcast.9, bf16[128,128]{1,0:T(8,128)(2,1)} %bitcast.10, bf16[128,128]{1,0:T(8,128)(2,1)} %bitcast.11, bf16[24576,128]{1,0:T(8,128)(2,1)} %bitcast.7, bf16[24576,128]{1,0:T(8,128)(2,1)} %bitcast.8, s32[1]{0:T(128)S(6)} %copy.8.plen_hbm), custom_call_target="tpu_custom_call" | custom-call | flops 12884901888 | bytes 12582912 | tf_op jit(solution)/shard_map/attend/pallas_call | solution.py:418
  38.8 0.8 %place.1 = (bf16[16,128,128]{2,1,0:T(8,128)(2,1)}, f32[16,128]{1,0:T(8,128)}) custom-call(bf16[16,128,128]{2,1,0:T(8,128)(2,1)S(1)} %bitcast.6, f32[8,1,256]{2,1,0:T(1,128)S(1)} %get-tuple-element.5.lse_ref), custom_call_target="tpu_custom_call" | custom-call | tf_op jit(solution)/shard_map/place/pallas_call | solution.py:429

commit v10 on v9

--- a/solution.py
+++ b/solution.py
@@ -89,8 +89,6 @@
     for e in range(2):
         mbuf[e][...] = jnp.full((8, rows), -3e38, F32)
 
-    pl.semaphore_wait(barrier, 3)
-
     def q_copy(k, h):
         peer, base = ((far_other, 3 * half), (far, 2 * half), (mate, half))[k]
         peer_core = (1 - core, core, 1 - core)[k]
@@ -98,10 +96,6 @@
             src_ref=q_hbm.at[:, half * peer_core + h], dst_ref=qraw.at[base + h],
             send_sem=q_send.at[k * half + h], recv_sem=q_recv.at[base + h],
             device_id={'cp': peer}, device_id_type=MESH)
-
-    for k in range(3):
-        for h in range(half):
-            q_copy(k, h).start()
 
     plen_copy.wait()
     visible_len = plen[0]
@@ -196,7 +190,11 @@
                 kbuf[h, pl.ds(base, PREP), :] = xk[h]
                 vbuf[h, :, pl.ds(base, PREP)] = xv[h].T
 
-        if j == 0:
+        if j == 2:
+            pl.semaphore_wait(barrier, 3)
+            for k in range(3):
+                for h in range(half):
+                    q_copy(k, h).start()
             kv_start(cache, dim)
         if j % 2 and j > 1:
             kv_start((j - 3) * raw_pos, 2 * raw_pos)

time: 39.7 us -> 39.2 us (0.987)
  Pallas kernels: 38.3 us -> 37.8 us
    pallas_call x1, Pallas kernels: 37.5 us -> 37 us  [local(): pl.pallas_call(attend_kernel, out_shape=(pltpu.VMEM((tok, kvh, ratio, dim...]
where the time goes in v10:
time: 39.2 us; the launch traced here: 39.1 us
  Pallas kernels  37.8 us (96%)
  between operations  1.29 us (3%)
    pallas_call x1, Pallas kernels, local(): pl.pallas_call(attend_kernel, out_shape=(pltpu.VMEM((tok, kvh, ratio, dim...  37 us
    pallas_call x1, Pallas kernels, local(): pl.pallas_call(place_kernel, out_shape=(jax.ShapeDtypeStruct((tok, heads,...  0.82 us

profile of v10, /device:TPU:0, one launch (start us, length us, event | category | flops | bytes accessed | tf_op | source)
XLA Modules:
  0.0 39.1 jit_solution(13082580594067074466)
XLA Ops:
  1.3 37.0 %attend.1 = (bf16[16,8,16,128]{3,2,1,0:T(8,128)(2,1)S(1)}, f32[8,1,256]{2,1,0:T(1,128)S(1)}) custom-call(bf16[16,8,16,128]{3,2,1,0:T(8,128)(2,1)} %bitcast.9, bf16[128,128]{1,0:T(8,128)(2,1)} %bitcast.10, bf16[128,128]{1,0:T(8,128)(2,1)} %bitcast.11, bf16[24576,128]{1,0:T(8,128)(2,1)} %bitcast.7, bf16[24576,128]{1,0:T(8,128)(2,1)} %bitcast.8, s32[1]{0:T(128)S(6)} %copy.8.plen_hbm), custom_call_target="tpu_custom_call" | custom-call | flops 12884901888 | bytes 12582912 | tf_op jit(solution)/shard_map/attend/pallas_call | solution.py:416
  38.3 0.8 %place.1 = (bf16[16,128,128]{2,1,0:T(8,128)(2,1)}, f32[16,128]{1,0:T(8,128)}) custom-call(bf16[16,128,128]{2,1,0:T(8,128)(2,1)S(1)} %bitcast.6, f32[8,1,256]{2,1,0:T(1,128)S(1)} %get-tuple-element.5.lse_ref), custom_call_target="tpu_custom_call" | custom-call | tf_op jit(solution)/shard_map/place/pallas_call | solution.py:427

commit v11 on v10

--- a/solution.py
+++ b/solution.py
@@ -14,8 +14,8 @@
 PREP = 128
 RAW_DEPTH = 3
 BF = jnp.bfloat16
-SEQ = ((0, 0), (2, 0), (4, 0), (12, 0), (14, 0), (12, 1), (8, 0), (14, 1),
-       (10, 0), (8, 1), (10, 1), (6, 0), (4, 1), (6, 1), (0, 1), (2, 1))
+SEQ = ((0, 0), (2, 0), (4, 0), (6, 0), (12, 0), (14, 0), (12, 1), (8, 0),
+       (14, 1), (10, 0), (8, 1), (10, 1), (4, 1), (6, 1), (0, 1), (2, 1))
 F32 = jnp.float32
 
 

time: 39.2 us -> 39.3 us (level)
  no operation moved by 1% of the time
where the time goes in v11:
time: 39.3 us; the launch traced here: 39.1 us
  Pallas kernels  37.9 us (96%)
  between operations  1.29 us (3%)
    pallas_call x1, Pallas kernels, local(): pl.pallas_call(attend_kernel, out_shape=(pltpu.VMEM((tok, kvh, ratio, dim...  37 us
    pallas_call x1, Pallas kernels, local(): pl.pallas_call(place_kernel, out_shape=(jax.ShapeDtypeStruct((tok, heads,...  0.82 us

profile of v11, /device:TPU:0, one launch (start us, length us, event | category | flops | bytes accessed | tf_op | source)
XLA Modules:
  0.0 39.1 jit_solution(11821287681815272094)
XLA Ops:
  1.3 37.0 %attend.1 = (bf16[16,8,16,128]{3,2,1,0:T(8,128)(2,1)S(1)}, f32[8,1,256]{2,1,0:T(1,128)S(1)}) custom-call(bf16[16,8,16,128]{3,2,1,0:T(8,128)(2,1)} %bitcast.9, bf16[128,128]{1,0:T(8,128)(2,1)} %bitcast.10, bf16[128,128]{1,0:T(8,128)(2,1)} %bitcast.11, bf16[24576,128]{1,0:T(8,128)(2,1)} %bitcast.7, bf16[24576,128]{1,0:T(8,128)(2,1)} %bitcast.8, s32[1]{0:T(128)S(6)} %copy.8.plen_hbm), custom_call_target="tpu_custom_call" | custom-call | flops 12884901888 | bytes 12582912 | tf_op jit(solution)/shard_map/attend/pallas_call | solution.py:416
  38.3 0.8 %place.1 = (bf16[16,128,128]{2,1,0:T(8,128)(2,1)}, f32[16,128]{1,0:T(8,128)}) custom-call(bf16[16,128,128]{2,1,0:T(8,128)(2,1)S(1)} %bitcast.6, f32[8,1,256]{2,1,0:T(1,128)S(1)} %get-tuple-element.5.lse_ref), custom_call_target="tpu_custom_call" | custom-call | tf_op jit(solution)/shard_map/place/pallas_call | solution.py:427

commit v12 on v10

--- a/solution.py
+++ b/solution.py
@@ -190,7 +190,7 @@
                 kbuf[h, pl.ds(base, PREP), :] = xk[h]
                 vbuf[h, :, pl.ds(base, PREP)] = xv[h].T
 
-        if j == 2:
+        if j == 1:
             pl.semaphore_wait(barrier, 3)
             for k in range(3):
                 for h in range(half):

time: 39.2 us -> 38.9 us (level)
  Pallas kernels: 37.8 us -> 37.4 us
where the time goes in v12:
time: 38.9 us; the launch traced here: 38.7 us
  Pallas kernels  37.4 us (96%)
  between operations  1.29 us (3%)
    pallas_call x1, Pallas kernels, local(): pl.pallas_call(attend_kernel, out_shape=(pltpu.VMEM((tok, kvh, ratio, dim...  36.6 us
    pallas_call x1, Pallas kernels, local(): pl.pallas_call(place_kernel, out_shape=(jax.ShapeDtypeStruct((tok, heads,...  0.82 us

profile of v12, /device:TPU:0, one launch (start us, length us, event | category | flops | bytes accessed | tf_op | source)
XLA Modules:
  0.0 38.7 jit_solution(9801768446302238579)
XLA Ops:
  1.3 36.6 %attend.1 = (bf16[16,8,16,128]{3,2,1,0:T(8,128)(2,1)S(1)}, f32[8,1,256]{2,1,0:T(1,128)S(1)}) custom-call(bf16[16,8,16,128]{3,2,1,0:T(8,128)(2,1)} %bitcast.9, bf16[128,128]{1,0:T(8,128)(2,1)} %bitcast.10, bf16[128,128]{1,0:T(8,128)(2,1)} %bitcast.11, bf16[24576,128]{1,0:T(8,128)(2,1)} %bitcast.7, bf16[24576,128]{1,0:T(8,128)(2,1)} %bitcast.8, s32[1]{0:T(128)S(6)} %copy.8.plen_hbm), custom_call_target="tpu_custom_call" | custom-call | flops 12884901888 | bytes 12582912 | tf_op jit(solution)/shard_map/attend/pallas_call | solution.py:416
  37.9 0.8 %place.1 = (bf16[16,128,128]{2,1,0:T(8,128)(2,1)}, f32[16,128]{1,0:T(8,128)}) custom-call(bf16[16,128,128]{2,1,0:T(8,128)(2,1)S(1)} %bitcast.6, f32[8,1,256]{2,1,0:T(1,128)S(1)} %get-tuple-element.5.lse_ref), custom_call_target="tpu_custom_call" | custom-call | tf_op jit(solution)/shard_map/place/pallas_call | solution.py:427

commit v13 on v12

--- a/solution.py
+++ b/solution.py
@@ -38,8 +38,8 @@
     return hit
 
 
-def attend_kernel(q_hbm, kn_hbm, vn_hbm, kc_hbm, vc_hbm, plen_hbm, out_ref, lse_ref,
-                  raw_k, raw_v, new_k, new_v, kbuf, vbuf, bias, qraw, qt, pick, plen, sbuf, mbuf,
+def attend_kernel(q_hbm, kn_hbm, vn_hbm, kc_hbm, vc_hbm, plen_ref, out_ref, lse_ref,
+                  raw_k, raw_v, new_k, new_v, kbuf, vbuf, bias, qraw, qt, pick, sbuf, mbuf,
                   st_o, st_m, st_l, ps, psl, pr, prl, fo, fl,
                   raw_sem, new_sem, q_send, q_recv, kv_send, k_recv, v_recv, p_send, p_recv, f_send, f_recv):
     tok, kvh, ratio, dim = q_hbm.shape
@@ -72,8 +72,6 @@
 
     for j in range(RAW_DEPTH):
         raw_start(j)
-    plen_copy = pltpu.make_async_copy(plen_hbm, plen, new_sem.at[2])
-    plen_copy.start()
     new_copies = (pltpu.make_async_copy(kn_hbm, new_k, new_sem.at[0]),
                   pltpu.make_async_copy(vn_hbm, new_v, new_sem.at[1]))
     for cp in new_copies:
@@ -97,8 +95,7 @@
             send_sem=q_send.at[k * half + h], recv_sem=q_recv.at[base + h],
             device_id={'cp': peer}, device_id_type=MESH)
 
-    plen_copy.wait()
-    visible_len = plen[0]
+    visible_len = plen_ref[0]
     for f, owner in enumerate((me, mate)):
         @pl.loop(0, chunks)
         def _(j):
@@ -397,7 +394,6 @@
             pltpu.VMEM((4 * half, tok, ratio, dim), BF),
             pltpu.VMEM((4 * half, dim, rows), BF),
             pltpu.VMEM((dim, rows), BF),
-            pltpu.SMEM((1,), jnp.int32),
             (pltpu.VMEM((cache + tok, rows), F32),) * 4,
             (pltpu.VMEM((8, rows), F32),) * 4,
             pltpu.VMEM((4 * half, dim, rows), F32),
@@ -409,14 +405,14 @@
             pltpu.VMEM((2 * half, 1, rows), F32),
             pltpu.VMEM((half, tok, ratio, dim), BF),
             pltpu.VMEM((half, 1, rows), F32),
-            dma((2, n_raw)), dma((3,)), dma((3 * half,)), dma((4 * half,)), dma((2, half)), dma((half,)), dma((half,)),
+            dma((2, n_raw)), dma((2,)), dma((3 * half,)), dma((4 * half,)), dma((2, half)), dma((half,)), dma((half,)),
             dma((2, 2 * half)), dma((2, 2 * half)), dma((2, half)), dma((2, half)),
         ]
         flops = 4 * heads * tok * 4 * cache * dim
         out, lse = pl.pallas_call(
             attend_kernel,
             out_shape=(pltpu.VMEM((tok, kvh, ratio, dim), BF), pltpu.VMEM((kvh, 1, rows), F32)),
-            in_specs=[hbm] * 6,
+            in_specs=[hbm] * 5 + [pl.BlockSpec(memory_space=pltpu.SMEM)],
             out_specs=(vmem, vmem),
             scratch_shapes=scratch,
             compiler_params=pltpu.CompilerParams(collective_id=0, has_side_effects=True, vmem_limit_bytes=60 * 2 ** 20),

time: 38.9 us -> 38.7 us (level)
  no operation moved by 1% of the time
where the time goes in v13:
time: 38.7 us; the launch traced here: 38.5 us
  Pallas kernels  37.2 us (96%)
  between operations  1.29 us (3%)
    pallas_call x1, Pallas kernels, local(): pl.pallas_call(attend_kernel, out_shape=(pltpu.VMEM((tok, kvh, ratio, dim...  36.4 us
    pallas_call x1, Pallas kernels, local(): pl.pallas_call(place_kernel, out_shape=(jax.ShapeDtypeStruct((tok, heads,...  0.82 us

profile of v13, /device:TPU:0, one launch (start us, length us, event | category | flops | bytes accessed | tf_op | source)
XLA Modules:
  0.0 38.5 jit_solution(12438473847685240640)
XLA Ops:
  1.3 36.4 %attend.1 = (bf16[16,8,16,128]{3,2,1,0:T(8,128)(2,1)S(1)}, f32[8,1,256]{2,1,0:T(1,128)S(1)}) custom-call(bf16[16,8,16,128]{3,2,1,0:T(8,128)(2,1)} %bitcast.9, bf16[128,128]{1,0:T(8,128)(2,1)} %bitcast.10, bf16[128,128]{1,0:T(8,128)(2,1)} %bitcast.11, bf16[24576,128]{1,0:T(8,128)(2,1)} %bitcast.7, bf16[24576,128]{1,0:T(8,128)(2,1)} %bitcast.8, s32[1]{0:T(128)S(6)} %copy.8.plen_ref), custom_call_target="tpu_custom_call" | custom-call | flops 12884901888 | bytes 12582912 | tf_op jit(solution)/shard_map/attend/pallas_call | solution.py:412
  37.7 0.8 %place.1 = (bf16[16,128,128]{2,1,0:T(8,128)(2,1)}, f32[16,128]{1,0:T(8,128)}) custom-call(bf16[16,128,128]{2,1,0:T(8,128)(2,1)S(1)} %bitcast.6, f32[8,1,256]{2,1,0:T(1,128)S(1)} %get-tuple-element.5.lse_ref), custom_call_target="tpu_custom_call" | custom-call | tf_op jit(solution)/shard_map/place/pallas_call | solution.py:423

commit v14 on v13

--- a/solution.py
+++ b/solution.py
@@ -70,8 +70,7 @@
         for cp in raw_copy(j):
             cp.start()
 
-    for j in range(RAW_DEPTH):
-        raw_start(j)
+    raw_start(0)
     new_copies = (pltpu.make_async_copy(kn_hbm, new_k, new_sem.at[0]),
                   pltpu.make_async_copy(vn_hbm, new_v, new_sem.at[1]))
     for cp in new_copies:
@@ -86,6 +85,7 @@
     pick[...] = jnp.where(lax.broadcasted_iota(jnp.int32, (dim, rows), 0) == 0, 1.0, 0.0).astype(BF)
     for e in range(2):
         mbuf[e][...] = jnp.full((8, rows), -3e38, F32)
+    raw_start(1)
 
     def q_copy(k, h):
         peer, base = ((far_other, 3 * half), (far, 2 * half), (mate, half))[k]
@@ -103,6 +103,9 @@
             pos = owner * cache + j * TK + lax.broadcasted_iota(jnp.int32, (TK, dim), 0)
             hidden = jnp.logical_and(lane == 0, pos >= visible_len)
             bias[f, pl.ds(pl.multiple_of(j * TK, TK), TK), :] = jnp.where(hidden, -BIG, 0.0).astype(BF)
+
+        if f == 0:
+            raw_start(2)
 
     for cp in new_copies:
         cp.wait()

time: 38.7 us -> 38.1 us (0.984)
  Pallas kernels: 37.2 us -> 36.6 us
    pallas_call x1, Pallas kernels: 36.4 us -> 35.8 us  [local(): pl.pallas_call(attend_kernel, out_shape=(pltpu.VMEM((tok, kvh, ratio, dim...]
where the time goes in v14:
time: 38.1 us; the launch traced here: 37.9 us
  Pallas kernels  36.6 us (96%)
  between operations  1.29 us (3%)
    pallas_call x1, Pallas kernels, local(): pl.pallas_call(attend_kernel, out_shape=(pltpu.VMEM((tok, kvh, ratio, dim...  35.8 us
    pallas_call x1, Pallas kernels, local(): pl.pallas_call(place_kernel, out_shape=(jax.ShapeDtypeStruct((tok, heads,...  0.82 us

profile of v14, /device:TPU:0, one launch (start us, length us, event | category | flops | bytes accessed | tf_op | source)
XLA Modules:
  0.0 37.9 jit_solution(11276872307950349645)
XLA Ops:
  1.3 35.8 %attend.1 = (bf16[16,8,16,128]{3,2,1,0:T(8,128)(2,1)S(1)}, f32[8,1,256]{2,1,0:T(1,128)S(1)}) custom-call(bf16[16,8,16,128]{3,2,1,0:T(8,128)(2,1)} %bitcast.9, bf16[128,128]{1,0:T(8,128)(2,1)} %bitcast.10, bf16[128,128]{1,0:T(8,128)(2,1)} %bitcast.11, bf16[24576,128]{1,0:T(8,128)(2,1)} %bitcast.7, bf16[24576,128]{1,0:T(8,128)(2,1)} %bitcast.8, s32[1]{0:T(128)S(6)} %copy.8.plen_ref), custom_call_target="tpu_custom_call" | custom-call | flops 12884901888 | bytes 12582912 | tf_op jit(solution)/shard_map/attend/pallas_call | solution.py:415
  37.1 0.8 %place.1 = (bf16[16,128,128]{2,1,0:T(8,128)(2,1)}, f32[16,128]{1,0:T(8,128)}) custom-call(bf16[16,128,128]{2,1,0:T(8,128)(2,1)S(1)} %bitcast.6, f32[8,1,256]{2,1,0:T(1,128)S(1)} %get-tuple-element.5.lse_ref), custom_call_target="tpu_custom_call" | custom-call | tf_op jit(solution)/shard_map/place/pallas_call | solution.py:426
